TPU v7x, 32 devices: a whole 2x2x4 slice. The times are simulated.
32 devices in a mesh: section: 16 (over z, x, core), dp: 2 (over y).
Axes of the slice: x: 2, y: 2, z: 4, core: 2. Of those that a mesh axis runs over, the one named last changes fastest.
Arguments:
- w_value: bfloat16 [16, 2, 4608, 1024], P('section', None, None, 'dp'), may hold values from -0.09375 to 0.09375
- w_out: bfloat16 [16, 2, 1024, 4608], P('section', None, 'dp'), may hold values from -0.1875 to 0.1875
- norm_gain: float32 [16, 2, 4608], P('section'), may hold values from 0.5 to 1.5
- saved_inputs: bfloat16 [16, 3, 2, 16, 4608], P('section', None, None, 'dp'), may hold values from -6 to 6
- arriving: bfloat16 [16, 2, 16, 4608], P('section', None, 'dp'), may hold values from -6 to 6
- returning: bfloat16 [16, 2, 16, 4608], P('section', None, 'dp'), may hold values from -6 to 6
- fresh_rows: bfloat16 [4, 16, 4608], P(None, 'dp'), may hold values from -6 to 6
- targets: bfloat16 [4, 16, 4608], P(None, 'dp'), may hold values from -6 to 6
- fill_slots: int32 [16, 4, 2], P('section'), may hold values from 0 to 2
- read_slots: int32 [16, 4, 2], P('section'), may hold values from 0 to 2
Outputs:
- activ_out: bfloat16 [16, 2, 16, 4608], P('section', None, 'dp')
- cotan_out: bfloat16 [16, 2, 16, 4608], P('section', None, 'dp')
- stash_out: bfloat16 [16, 3, 2, 16, 4608], P('section', None, None, 'dp')
- grad_value: bfloat16 [16, 2, 4608, 1024], P('section', None, None, 'dp')
- grad_out: bfloat16 [16, 2, 1024, 4608], P('section', None, 'dp')
- grad_gain: float32 [16, 2, 4608], P('section')
All inputs are finite; a program needn't handle non-finite values.
Results may differ from a plain program's by a relative error of at most 0.029.
Values may be sent and summed in bfloat16 or wider, within the bound.
A program may use at most 192 MiB of HBM per device.

v0:
```python
import functools

import jax
import jax.numpy as jnp
from jax import lax
from jax.experimental import pallas as pl
from jax.experimental.pallas import tpu as pltpu
from jax.sharding import PartitionSpec as P

epsilon = 1e-06


def shifted(shard, axis, by):
    devices = lax.axis_size(axis)
    return lax.ppermute(shard, axis, [(i, (i + by) % devices) for i in range(devices)])


def normalize(block_rows, gain_row):
    values = block_rows.astype(jnp.float32)
    inv_root = lax.rsqrt(jnp.mean(values * values, axis=-1, keepdims=True) + epsilon)
    scaled = values * inv_root
    return (scaled, inv_root, (scaled * gain_row).astype(jnp.bfloat16))


def times_transposed(left, right):
    return lax.dot_general(
        left, right, (((1,), (1,)), ((), ())), preferred_element_type=jnp.float32
    )


def transposed_times(left, right):
    return lax.dot_general(
        left, right, (((0,), (0,)), ((), ())), preferred_element_type=jnp.float32
    )


def weight_terms(value_group, normed_all, down_grad, upstream_all):
    values = jnp.dot(normed_all, value_group, preferred_element_type=jnp.float32).astype(
        jnp.bfloat16
    )
    return (transposed_times(normed_all, down_grad), transposed_times(values, upstream_all))


def body(
    w_value,
    w_out,
    norm_gain,
    saved_inputs,
    arriving,
    returning,
    fresh_rows,
    targets,
    fill_slots,
    read_slots,
):
    value_mats = w_value[0]
    out_mats = w_out[0]
    gains = norm_gain[0]
    saved = saved_inputs[0]
    activations = arriving[0]
    cotangents = returning[0]
    tick_count = fresh_rows.shape[0]
    tok_rows = activations.shape[1]
    all_rows = tok_rows * lax.axis_size("dp")
    section_index = lax.axis_index("section")
    last_section = lax.axis_size("section") - 1
    row_offset = lax.axis_index("dp") * tok_rows
    activations, new_rows = (
        lax.all_gather(activations, "dp", axis=1, tiled=True),
        lax.all_gather(fresh_rows, "dp", axis=1, tiled=True),
    )

    def own_rows(block):
        return lax.dynamic_slice_in_dim(block, row_offset, tok_rows, 0)

    def forward(block, group):
        scaled, inv_root, normed = normalize(block, gains[group])
        values = jnp.dot(normed, value_mats[group], preferred_element_type=jnp.float32).astype(
            jnp.bfloat16
        )
        summed = lax.psum(
            jnp.dot(values, out_mats[group], preferred_element_type=jnp.float32).astype(
                jnp.bfloat16
            ),
            "dp",
        ).astype(jnp.float32)
        return (block.astype(jnp.float32) + summed).astype(jnp.bfloat16)

    value_sums = [jnp.zeros(value_mats.shape[1:], jnp.float32) for group in range(2)]
    out_sums = [jnp.zeros(out_mats.shape[1:], jnp.float32) for group in range(2)]
    gain_sums = [jnp.zeros(gains.shape[1:], jnp.float32) for group in range(2)]
    outputs = activations
    gradients = cotangents
    for tick_index in range(tick_count):
        if tick_index > 0:
            received = shifted(outputs, "section", 1)
            lower_group = jnp.where(section_index == 0, new_rows[tick_index], received[0])
            upper_group = jnp.where(section_index == 0, received[0], received[1])
            activations = jnp.stack([lower_group, upper_group])
            returned = shifted(gradients, "section", -1)
            finish = (
                own_rows(outputs[1]).astype(jnp.float32)
                - targets[tick_index - 1].astype(jnp.float32)
            ).astype(jnp.bfloat16)
            cotangents = jnp.stack(
                [
                    jnp.where(section_index == last_section, returned[1], returned[0]),
                    jnp.where(section_index == last_section, finish, returned[1]),
                ]
            )
        for group in range(2):
            saved = saved.at[fill_slots[0, tick_index, group], group].set(
                own_rows(activations[group])
            )
        outputs = jnp.stack([forward(activations[0], 0), forward(activations[1], 1)])
        fresh_grads = []
        for group in range(2):
            source = saved[read_slots[0, tick_index, group], group]
            scaled, inv_root, normed = normalize(source, gains[group])
            normed_all, upstream_all = (
                lax.all_gather(normed, "dp", axis=0, tiled=True),
                lax.all_gather(cotangents[group], "dp", axis=0, tiled=True),
            )
            down_grad = times_transposed(upstream_all, out_mats[group]).astype(jnp.bfloat16)
            pulled = lax.psum_scatter(
                times_transposed(down_grad, value_mats[group]).astype(jnp.bfloat16),
                "dp",
                scatter_dimension=0,
                tiled=True,
            ).astype(jnp.float32)
            weighted = pulled * gains[group]
            inner_mean = jnp.mean(weighted * scaled, axis=-1, keepdims=True)
            fresh_grads.append(
                (
                    cotangents[group].astype(jnp.float32)
                    + inv_root * (weighted - scaled * inner_mean)
                ).astype(jnp.bfloat16)
            )
            gain_sums[group] = gain_sums[group] + jnp.sum(pulled * scaled, axis=0)
            value_term, out_term = weight_terms(
                value_mats[group], normed_all, down_grad, upstream_all
            )
            value_sums[group] = value_sums[group] + value_term
            out_sums[group] = out_sums[group] + out_term
        gradients = jnp.stack(fresh_grads)
    grad_scale = (tick_count * all_rows) ** (-0.5)
    gain_total = lax.psum(jnp.stack(gain_sums).astype(jnp.bfloat16), "dp").astype(jnp.float32)
    final_rows = jnp.stack([own_rows(outputs[0]), own_rows(outputs[1])])
    return (
        final_rows[None],
        gradients[None],
        saved[None],
        (jnp.stack(value_sums) * grad_scale).astype(jnp.bfloat16)[None],
        (jnp.stack(out_sums) * grad_scale).astype(jnp.bfloat16)[None],
        (gain_total * grad_scale)[None],
    )


CHUNK = 512
VMEM_GRANT = 60 * 1024 * 1024
MESH = pl.DeviceIdType.MESH


def chunk_loop(width, step):
    size = CHUNK if width % CHUNK == 0 else width
    lax.fori_loop(0, width // size, lambda i, _: step(pl.ds(pl.multiple_of(i * size, size), size)), None, unroll=UNROLL)


UNROLL = 9


def contract_sum(width, term, shape):
    size = CHUNK if width % CHUNK == 0 else width

    def step(i, total):
        return total + term(pl.ds(pl.multiple_of(i * size, size), size))

    return lax.fori_loop(0, width // size, step, jnp.zeros(shape, jnp.float32), unroll=UNROLL)


def relay_kernel(
    sections,
    wv_hbm,
    wo_hbm,
    gain_ref,
    saved_ref,
    arriving_ref,
    returning_ref,
    fresh_ref,
    targets_ref,
    fill_ref,
    read_ref,
    activ_ref,
    cotan_ref,
    stash_out_ref,
    normed_ref,
    down_ref,
    vals_ref,
    up_ref,
    gain_out_ref,
    wv,
    wo,
    xin,
    cot,
    stash,
    tgt,
    psend,
    precv,
    moved,
    lhs,
    w_sem,
    init_send,
    init_recv,
    ex_send,
    ex_recv,
    sh_send,
    sh_recv,
):
    s = lax.axis_index("section")
    d = lax.axis_index("dp")
    peer = 1 - d
    after = lax.rem(s + 1, sections)
    before = lax.rem(s + sections - 1, sections)
    is_last = s // (sections - 1)
    is_first = before // (sections - 1)
    ticks = fresh_ref.shape[0]
    half, width = arriving_ref.shape[1:]
    rows = 2 * half
    features = wv.shape[2]
    slots = saved_ref.shape[0]

    weight_copies = []
    for group in range(2):
        weight_copies.append(pltpu.make_async_copy(wv_hbm.at[group], wv.at[group], w_sem.at[group, 0]))
        weight_copies.append(pltpu.make_async_copy(wo_hbm.at[group], wo.at[group], w_sem.at[group, 1]))
    for copy in weight_copies:
        copy.start()

    barrier = pltpu.get_barrier_semaphore()
    for target in ((s, peer), (after, d), (before, d)):
        pl.semaphore_signal(barrier, inc=1, device_id=target, device_id_type=MESH)
    pl.semaphore_wait(barrier, 3)

    def to_peer(src, dst, send, recv):
        return pltpu.make_async_remote_copy(
            src_ref=src, dst_ref=dst, send_sem=send, recv_sem=recv,
            device_id=(s, peer), device_id_type=MESH,
        )

    def initial(index, src, dst):
        return to_peer(src, dst, init_send.at[index], init_recv.at[index])

    first_in = initial(0, arriving_ref, xin.at[0, pl.ds(0, 2), d])
    first_cot = initial(1, returning_ref, cot.at[0, pl.ds(0, 2), d])
    first_stash = initial(2, saved_ref, stash.at[:, :, d])
    fresh_copy = initial(3, fresh_ref.at[pl.ds(1, ticks - 1)], xin.at[pl.ds(1, ticks - 1), 2, d])
    target_copy = initial(4, targets_ref, tgt.at[:, d])
    first_in.start()
    first_cot.start()

    @pl.when(s == 0)
    def _():
        fresh_copy.start()

    @pl.when(s == sections - 1)
    def _():
        target_copy.start()

    first_stash.start()
    for group in range(2):
        xin[0, group, d] = arriving_ref[group]
        cot[0, group, d] = returning_ref[group]
        for slot in range(slots):
            stash[slot, group, d] = saved_ref[slot, group]
    for tick in range(1, ticks):
        xin[tick, 2, d] = fresh_ref[tick]
    for tick in range(ticks):
        tgt[tick, d] = targets_ref[tick]
    gain_out_ref[...] = jnp.zeros_like(gain_out_ref)

    def whole(block):
        return block.astype(jnp.float32).reshape(rows, width)

    def parted(block):
        return block.reshape(2, half, width).astype(jnp.bfloat16)

    def exchange(tick, stream):
        return to_peer(
            psend.at[tick, stream], precv.at[tick, stream],
            ex_send.at[tick, stream], ex_recv.at[tick, stream],
        )

    def shift(tick, stream):
        group = stream % 2
        if stream < 2:
            place, target, buffer = (group + is_last) % 2, after, xin
        else:
            place, target, buffer = (group + is_first) % 2, before, cot
        return pltpu.make_async_remote_copy(
            src_ref=moved.at[tick, stream], dst_ref=buffer.at[tick + 1, place],
            send_sem=sh_send.at[tick, stream], recv_sem=sh_recv.at[tick + 1, stream - group + place],
            device_id=(target, d), device_id_type=MESH,
        )

    def shift_arrival(tick, stream):
        buffer = xin if stream < 2 else cot
        return pltpu.make_async_remote_copy(
            src_ref=moved.at[0, stream], dst_ref=buffer.at[tick, stream % 2],
            send_sem=sh_send.at[0, stream], recv_sem=sh_recv.at[tick, stream],
            device_id=(after, d), device_id_type=MESH,
        )

    def input_block(tick, group):
        return whole(xin[tick, 2 * is_first if group == 0 else 1])

    def cot_block(tick, group):
        return whole(cot[tick, 0 if group == 0 else 1 + is_last])

    def norm_parts(values, group):
        inv_root = lax.rsqrt(jnp.mean(values * values, axis=-1, keepdims=True) + epsilon)
        scaled = values * inv_root
        return scaled, inv_root, (scaled * gain_ref[pl.ds(group, 1), :]).astype(jnp.bfloat16)

    def value_product(rows_of, group):
        return contract_sum(
            width,
            lambda at: jnp.dot(rows_of(at), wv[group, at, :], preferred_element_type=jnp.float32),
            (rows, features),
        ).astype(jnp.bfloat16)

    def arrive(tick, stream):
        @pl.when(tick > 0)
        def _():
            shift_arrival(tick, stream).wait_recv()

    def weights_ready(tick, index):
        @pl.when(tick == 0)
        def _():
            weight_copies[index].wait()

    def forward_start(tick, group):
        arrive(tick, group)
        lhs[...] = norm_parts(input_block(tick, group), group)[2]
        weights_ready(tick, 2 * group)
        values = value_product(lambda at: lhs[:, at], group)
        weights_ready(tick, 2 * group + 1)

        def step(at):
            psend[tick, group, :, at] = jnp.dot(
                values, wo[group, :, at], preferred_element_type=jnp.float32
            ).astype(jnp.bfloat16)

        chunk_loop(width, step)
        exchange(tick, group).start()

    def send_on(tick, stream):
        @pl.when(tick < ticks - 1)
        def _():
            shift(tick, stream).start()

    def peer_sum(tick, stream):
        exchange(tick, stream).wait_recv()
        return psend[tick, stream].astype(jnp.float32) + precv[tick, stream].astype(jnp.float32)

    def forward_finish(tick, group):
        outputs = parted(input_block(tick, group) + peer_sum(tick, group))
        moved[tick, group] = outputs
        send_on(tick, group)
        if group == 1:
            @pl.when((tick < ticks - 1) & (s == sections - 1))
            def _():
                cot[tick + 1, 2] = (
                    outputs.astype(jnp.float32) - tgt[tick].astype(jnp.float32)
                ).astype(jnp.bfloat16)

    def backward_start(tick, group):
        arrive(tick, 2 + group)
        up_ref[group, tick] = cot_block(tick, group).astype(jnp.bfloat16)
        down = contract_sum(
            width,
            lambda at: times_transposed(up_ref[group, tick, :, at], wo[group, :, at]),
            (rows, features),
        ).astype(jnp.bfloat16)
        down_ref[group, tick] = down

        def step(at):
            psend[tick, 2 + group, :, at] = times_transposed(down, wv[group, at, :]).astype(
                jnp.bfloat16
            )

        chunk_loop(width, step)
        exchange(tick, 2 + group).start()

    def stash_step(tick, group):
        block = xin[tick, 2 * is_first if group == 0 else 1]
        for slot in range(slots):
            stash[slot, group] = jnp.where(fill_ref[tick, group] == slot, block, stash[slot, group])

    def source_values(tick, group):
        normed_ref[group, tick] = norm_parts(whole(stash[read_ref[tick, group], group]), group)[2]
        vals_ref[group, tick] = value_product(lambda at: normed_ref[group, tick, :, at], group)

    def backward_finish(tick, group):
        scaled, inv_root, _ = norm_parts(whole(stash[read_ref[tick, group], group]), group)
        pulled = peer_sum(tick, 2 + group)
        weighted = pulled * gain_ref[pl.ds(group, 1), :]
        inner_mean = jnp.mean(weighted * scaled, axis=-1, keepdims=True)
        moved[tick, 2 + group] = parted(
            cot_block(tick, group) + inv_root * (weighted - scaled * inner_mean)
        )
        send_on(tick, 2 + group)
        gain_out_ref[pl.ds(group, 1), :] += jnp.sum(pulled * scaled, axis=0, keepdims=True)

    first_in.wait_recv()
    xin[0, 2] = xin[0, 0]

    @pl.when(s == 0)
    def _():
        fresh_copy.wait()

    @pl.when(s == sections - 1)
    def _():
        target_copy.wait()

    def tick_step(tick, _):
        forward_start(tick, 0)
        forward_start(tick, 1)
        forward_finish(tick, 0)

        @pl.when(tick == 0)
        def _():
            first_cot.wait_recv()
            cot[0, 2] = cot[0, 1]

        backward_start(tick, 0)
        forward_finish(tick, 1)

        @pl.when(tick == 0)
        def _():
            first_stash.wait_recv()

        stash_step(tick, 0)
        stash_step(tick, 1)
        backward_start(tick, 1)
        backward_finish(tick, 0)
        source_values(tick, 0)
        source_values(tick, 1)
        backward_finish(tick, 1)
        return None

    lax.fori_loop(0, ticks, tick_step, None)

    for group in range(2):
        activ_ref[group] = moved[ticks - 1, group, d]
        cotan_ref[group] = moved[ticks - 1, 2 + group, d]
        for slot in range(slots):
            stash_out_ref[slot, group] = stash[slot, group, d]
    gain_out_ref[...] = gain_out_ref[...] * (ticks * rows) ** (-0.5)
    for copy in (first_in, first_cot, first_stash):
        copy.wait_send()
    for tick in range(ticks):
        for stream in range(4):
            exchange(tick, stream).wait_send()
            if tick < ticks - 1:
                shift(tick, stream).wait_send()


def relay_body(
    sections,
    w_value,
    w_out,
    norm_gain,
    saved_inputs,
    arriving,
    returning,
    fresh_rows,
    targets,
    fill_slots,
    read_slots,
):
    value_mats, out_mats, gains = w_value[0], w_out[0], norm_gain[0]
    saved, activations, cotangents = saved_inputs[0], arriving[0], returning[0]
    ticks, half, width = fresh_rows.shape
    features = value_mats.shape[2]
    slots = saved.shape[0]
    rows = 2 * half
    vmem = pl.BlockSpec(memory_space=pltpu.VMEM)
    smem = pl.BlockSpec(memory_space=pltpu.SMEM)
    hbm = pl.BlockSpec(memory_space=pl.ANY)
    shape = jax.ShapeDtypeStruct
    narrow = jnp.bfloat16
    final_rows, gradients, stash_rows, normed, down, values, upstream, gain_sums = pl.pallas_call(
        functools.partial(relay_kernel, sections),
        out_shape=(
            shape(activations.shape, narrow),
            shape(cotangents.shape, narrow),
            shape(saved.shape, narrow),
            shape((2, ticks, rows, width), narrow),
            shape((2, ticks, rows, features), narrow),
            shape((2, ticks, rows, features), narrow),
            shape((2, ticks, rows, width), narrow),
            shape(gains.shape, jnp.float32),
        ),
        in_specs=[hbm, hbm] + [vmem] * 6 + [smem] * 2,
        out_specs=(vmem,) * 8,
        scratch_shapes=[
            pltpu.VMEM(value_mats.shape, narrow),
            pltpu.VMEM(out_mats.shape, narrow),
            pltpu.VMEM((ticks, 3, 2, half, width), narrow),
            pltpu.VMEM((ticks, 3, 2, half, width), narrow),
            pltpu.VMEM((slots, 2, 2, half, width), narrow),
            pltpu.VMEM((ticks, 2, half, width), narrow),
            pltpu.VMEM((ticks, 4, rows, width), narrow),
            pltpu.VMEM((ticks, 4, rows, width), narrow),
            pltpu.VMEM((ticks, 4, 2, half, width), narrow),
            pltpu.VMEM((rows, width), narrow),
            pltpu.SemaphoreType.DMA((2, 2)),
            pltpu.SemaphoreType.DMA((5,)),
            pltpu.SemaphoreType.DMA((5,)),
            pltpu.SemaphoreType.DMA((ticks, 4)),
            pltpu.SemaphoreType.DMA((ticks, 4)),
            pltpu.SemaphoreType.DMA((ticks, 4)),
            pltpu.SemaphoreType.DMA((ticks, 4)),
        ],
        compiler_params=pltpu.CompilerParams(
            collective_id=0, has_side_effects=True, vmem_limit_bytes=VMEM_GRANT
        ),
    )(
        value_mats, out_mats, gains, saved, activations, cotangents,
        fresh_rows, targets, fill_slots[0], read_slots[0],
    )
    grad_scale = (ticks * rows) ** (-0.5)

    def weight_grad(left, right):
        flat = lambda block: block.reshape(2, ticks * rows, block.shape[3])
        total = lax.dot_general(
            flat(left), flat(right), (((1,), (1,)), ((0,), (0,))), preferred_element_type=jnp.float32
        )
        return (total * grad_scale).astype(jnp.bfloat16)[None]

    return (
        final_rows[None],
        gradients[None],
        stash_rows[None],
        weight_grad(normed, down),
        weight_grad(values, upstream),
        gain_sums[None],
    )


def solution(mesh):
    in_specs = (
        P("section", None, None, "dp"),
        P("section", None, "dp", None),
        P("section", None, None),
        P("section", None, None, "dp", None),
        P("section", None, "dp", None),
        P("section", None, "dp", None),
        P(None, "dp", None),
        P(None, "dp", None),
        P("section", None, None),
        P("section", None, None),
    )
    out_specs = (
        P("section", None, "dp", None),
        P("section", None, "dp", None),
        P("section", None, None, "dp", None),
        P("section", None, None, "dp"),
        P("section", None, "dp", None),
        P("section", None, None),
    )
    paired = mesh.shape["dp"] == 2 and mesh.shape["section"] > 2
    program = functools.partial(relay_body, mesh.shape["section"]) if paired else body
    return jax.shard_map(program, mesh=mesh, in_specs=in_specs, out_specs=out_specs, check_vma=False)
```

profile of v0, /device:TPU:0, one launch (start us, length us, event | category | flops | bytes accessed | tf_op | source)
XLA Modules:
  0.0 118.3 jit_solution(442377884616358801)
XLA Ops:
  0.6 1.3 %copy.16.fill_ref = s32[4,2]{1,0:T(4,128)} copy(s32[4,2]{0,1:T(2,128)} %bitcast.38) | data formatting | bytes 64 | tf_op jit(solution)/shard_map/squeeze | solution.py:530
  2.0 1.3 %copy.17.read_ref = s32[4,2]{1,0:T(4,128)} copy(s32[4,2]{0,1:T(2,128)} %bitcast.39) | data formatting | bytes 64 | tf_op jit(solution)/shard_map/squeeze | solution.py:530
  3.3 99.2 %shard_map.145 = (bf16[2,8,4608]{2,1,0:T(8,128)(2,1)}, bf16[2,8,4608]{2,1,0:T(8,128)(2,1)}, bf16[3,2,8,4608]{3,2,1,0:T(8,128)(2,1)}, bf16[2,4,16,4608]{3,2,1,0:T...) custom-call(bf16[2,4608,512]{2,1,0:T(8,128)(2,1)} %bitcast.24, ...), custom_call_target="tpu_custom_call" | custom-call | tf_op jit(solution)/shard_map/pallas_call | solution.py:492
  102.5 0.0 copy-start
  102.6 0.0 copy-start.4
  102.6 0.0 copy-start.3
  102.6 0.0 copy-start.2
  102.6 0.0 copy-start.1
  102.6 0.0 copy-start.5
  102.6 7.8 %fusion = bf16[1,2,4608,512]{3,2,1,0:T(8,128)(2,1)} fusion(bf16[2,64,4608]{2,1,0:T(8,128)(2,1)} %bitcast.27, bf16[2,64,512]{2,1,0:T(8,128)(2,1)} %bitcast.35), kind=kOutput, calls=%fused_computation.2 | convolution fusion | flops 613416960 | bytes 10747904 | tf_op jit(solution)/shard_map/dot_general | solution.py:536
  110.4 0.0 copy-done
  110.4 0.0 copy-done.4
  110.4 5.2 %fusion.1 = bf16[1,2,512,4608]{3,2,1,0:T(8,128)(2,1)} fusion(bf16[2,64,512]{2,1,0:T(8,128)(2,1)S(1)} %bitcast.34, bf16[2,64,4608]{2,1,0:T(8,128)(2,1)S(1)} %bitcast.26), kind=kOutput, calls=%fused_computation.3 | convolution fusion | flops 613416960 | bytes 10747904 | tf_op jit(solution)/shard_map/dot_general | solution.py:536
  115.6 0.0 copy-done.3
  115.6 0.7 copy.22
  116.2 0.0 copy-done.2
  116.2 0.7 copy.23
  116.9 0.0 copy-done.1
  116.9 0.8 copy.24
  117.7 0.0 copy-done.5
  117.7 0.6 copy.25
Async XLA Ops:
  102.5 7.9 %copy-start = (bf16[2,4,16,4608]{3,2,1,0:T(8,128)(2,1)S(1)}, bf16[2,4,16,4608]{3,2,1,0:T(8,128)(2,1)}, u32[]{:S(2)}) copy-start(bf16[2,4,16,4608]{3,2,1,0:T(8,128)(2,1)} %get-tuple-element.20) | copy-start | bytes 3538948
  102.6 7.9 %copy-start.4 = (bf16[2,4,16,512]{3,2,1,0:T(8,128)(2,1)S(1)}, bf16[2,4,16,512]{3,2,1,0:T(8,128)(2,1)}, u32[]{:S(2)}) copy-start(bf16[2,4,16,512]{3,2,1,0:T(8,128)(2,1)} %get-tuple-element.19) | copy-start | bytes 393220
  102.6 13.0 %copy-start.3 = (bf16[2,8,4608]{2,1,0:T(8,128)(2,1)S(1)}, bf16[2,8,4608]{2,1,0:T(8,128)(2,1)}, u32[]{:S(2)}) copy-start(bf16[2,8,4608]{2,1,0:T(8,128)(2,1)} %get-tuple-element.14) | copy-start | bytes 442372
  102.6 13.7 %copy-start.2 = (bf16[2,8,4608]{2,1,0:T(8,128)(2,1)S(1)}, bf16[2,8,4608]{2,1,0:T(8,128)(2,1)}, u32[]{:S(2)}) copy-start(bf16[2,8,4608]{2,1,0:T(8,128)(2,1)} %get-tuple-element.15) | copy-start | bytes 442372
  102.6 14.3 %copy-start.1 = (bf16[3,2,8,4608]{3,2,1,0:T(8,128)(2,1)S(1)}, bf16[3,2,8,4608]{3,2,1,0:T(8,128)(2,1)}, u32[]{:S(2)}) copy-start(bf16[3,2,8,4608]{3,2,1,0:T(8,128)(2,1)} %get-tuple-element.16) | copy-start | bytes 1327108
  102.6 15.1 %copy-start.5 = (f32[2,4608]{1,0:T(2,128)S(1)}, f32[2,4608]{1,0:T(2,128)}, u32[]{:S(2)}) copy-start(f32[2,4608]{1,0:T(2,128)} %get-tuple-element.21) | copy-start | bytes 110596
where the time goes:
time: 118 us
  Pallas kernels  99.2 us (84%)
  matrix products  13 us (11%)
  local copies, waits for them, and re-layouts  5.4 us (5%)
    pallas_call x1, Pallas kernels, relay_body(): pl.pallas_call(functools.partial(relay_kernel, sections), out_shape=(shap...  99.2 us
    dot_general x2, matrix products, weight_grad(): lax.dot_general(flat(left), flat(right), (((1,), (1,)), ((0,), (0,))), pr...  13 us
    unnamed x16, local copies, waits for them, and re-layouts  2.73 us

commit v1 on v0

--- a/solution.py
+++ b/solution.py
@@ -394,14 +394,14 @@
     def stash_step(tick, group):
         block = xin[tick, 2 * is_first if group == 0 else 1]
         for slot in range(slots):
-            stash[slot, group] = jnp.where(fill_ref[tick, group] == slot, block, stash[slot, group])
+            stash[slot, group] = jnp.where(fill_ref[group, tick] == slot, block, stash[slot, group])
 
     def source_values(tick, group):
-        normed_ref[group, tick] = norm_parts(whole(stash[read_ref[tick, group], group]), group)[2]
+        normed_ref[group, tick] = norm_parts(whole(stash[read_ref[group, tick], group]), group)[2]
         vals_ref[group, tick] = value_product(lambda at: normed_ref[group, tick, :, at], group)
 
     def backward_finish(tick, group):
-        scaled, inv_root, _ = norm_parts(whole(stash[read_ref[tick, group], group]), group)
+        scaled, inv_root, _ = norm_parts(whole(stash[read_ref[group, tick], group]), group)
         pulled = peer_sum(tick, 2 + group)
         weighted = pulled * gain_ref[pl.ds(group, 1), :]
         inner_mean = jnp.mean(weighted * scaled, axis=-1, keepdims=True)
@@ -463,6 +463,46 @@
             exchange(tick, stream).wait_send()
             if tick < ticks - 1:
                 shift(tick, stream).wait_send()
+
+
+def grads_kernel(
+    grad_scale, activ_ref, cotan_ref, stash_ref, gain_ref, normed_ref, down_ref, vals_ref, up_ref,
+    activ_hbm, cotan_hbm, stash_hbm, value_hbm, out_hbm, gain_hbm,
+    value_grad, out_grad, small_sem, grad_sem,
+):
+    small = [
+        pltpu.make_async_copy(source, target, small_sem.at[index])
+        for index, (source, target) in enumerate(
+            ((activ_ref, activ_hbm), (cotan_ref, cotan_hbm), (stash_ref, stash_hbm), (gain_ref, gain_hbm))
+        )
+    ]
+    for copy in small:
+        copy.start()
+    width = normed_ref.shape[2]
+    size = CHUNK if width % CHUNK == 0 else width
+
+    def step(index, _):
+        at = pl.ds(pl.multiple_of(index * size, size), size)
+        for group in range(2):
+            value_grad[group, at, :] = (
+                transposed_times(normed_ref[group, :, at], down_ref[group]) * grad_scale
+            ).astype(jnp.bfloat16)
+            pltpu.make_async_copy(
+                value_grad.at[group, at, :], value_hbm.at[group, at, :], grad_sem.at[0]
+            ).start()
+            out_grad[group, :, at] = (
+                transposed_times(vals_ref[group], up_ref[group, :, at]) * grad_scale
+            ).astype(jnp.bfloat16)
+            pltpu.make_async_copy(
+                out_grad.at[group, :, at], out_hbm.at[group, :, at], grad_sem.at[1]
+            ).start()
+        return None
+
+    lax.fori_loop(0, width // size, step, None)
+    pltpu.make_async_copy(value_grad, value_hbm, grad_sem.at[0]).wait()
+    pltpu.make_async_copy(out_grad, out_hbm, grad_sem.at[1]).wait()
+    for copy in small:
+        copy.wait()
 
 
 def relay_body(
@@ -527,25 +567,30 @@
         ),
     )(
         value_mats, out_mats, gains, saved, activations, cotangents,
-        fresh_rows, targets, fill_slots[0], read_slots[0],
-    )
-    grad_scale = (ticks * rows) ** (-0.5)
-
-    def weight_grad(left, right):
-        flat = lambda block: block.reshape(2, ticks * rows, block.shape[3])
-        total = lax.dot_general(
-            flat(left), flat(right), (((1,), (1,)), ((0,), (0,))), preferred_element_type=jnp.float32
-        )
-        return (total * grad_scale).astype(jnp.bfloat16)[None]
-
-    return (
-        final_rows[None],
-        gradients[None],
-        stash_rows[None],
-        weight_grad(normed, down),
-        weight_grad(values, upstream),
-        gain_sums[None],
-    )
+        fresh_rows, targets, fill_slots[0].T, read_slots[0].T,
+    )
+    flat = lambda block: block.reshape(2, ticks * rows, block.shape[3])
+    grads = pl.pallas_call(
+        functools.partial(grads_kernel, (ticks * rows) ** (-0.5)),
+        out_shape=(
+            shape(activations.shape, narrow),
+            shape(cotangents.shape, narrow),
+            shape(saved.shape, narrow),
+            shape(value_mats.shape, narrow),
+            shape(out_mats.shape, narrow),
+            shape(gains.shape, jnp.float32),
+        ),
+        in_specs=[vmem] * 8,
+        out_specs=(hbm,) * 6,
+        scratch_shapes=[
+            pltpu.VMEM(value_mats.shape, narrow),
+            pltpu.VMEM(out_mats.shape, narrow),
+            pltpu.SemaphoreType.DMA((4,)),
+            pltpu.SemaphoreType.DMA((2,)),
+        ],
+        compiler_params=pltpu.CompilerParams(vmem_limit_bytes=VMEM_GRANT),
+    )(final_rows, gradients, stash_rows, gain_sums, flat(normed), flat(down), flat(values), flat(upstream))
+    return tuple(block[None] for block in grads)
 
 
 def solution(mesh):

time: 118 us -> 110 us (0.932)
  matrix products: 13 us -> 0 us
  Pallas kernels: 99.2 us -> 109 us
  local copies, waits for them, and re-layouts: 5.4 us -> 0 us
    dot_general x2 -> x0, matrix products: 13 us -> none  [weight_grad(): lax.dot_general(flat(left), flat(right), (((1,), (1,)), ((0,), (0,))), pr...]
    pallas_call x0 -> x1, Pallas kernels: none -> 9.63 us  [relay_body(): pl.pallas_call(functools.partial(grads_kernel, (ticks * rows) ** (-0.5)),...]
    unnamed x16 -> x0, local copies, waits for them, and re-layouts: 2.73 us -> none
    squeeze x2 -> x0, local copies, waits for them, and re-layouts: 2.67 us -> none  [the longest x1 1.34 us: relay_body(): fill_slots[0]]
where the time goes in v1:
time: 110 us
  Pallas kernels  109 us (99%)
    pallas_call x1, Pallas kernels, relay_body(): pl.pallas_call(functools.partial(relay_kernel, sections), out_shape=(shap...  99.3 us
    pallas_call x1, Pallas kernels, relay_body(): pl.pallas_call(functools.partial(grads_kernel, (ticks * rows) ** (-0.5)),...  9.63 us

profile of v1, /device:TPU:0, one launch (start us, length us, event | category | flops | bytes accessed | tf_op | source)
XLA Modules:
  0.0 109.6 jit_solution(3006945517593966042)
XLA Ops:
  0.6 99.3 %shard_map.145 = (bf16[2,8,4608]{2,1,0:T(8,128)(2,1)}, bf16[2,8,4608]{2,1,0:T(8,128)(2,1)}, bf16[3,2,8,4608]{3,2,1,0:T(8,128)(2,1)}, bf16[2,4,16,4608]{3,2,1,0:T...) custom-call(bf16[2,4608,512]{2,1,0:T(8,128)(2,1)} %bitcast.22, ...), custom_call_target="tpu_custom_call" | custom-call | tf_op jit(solution)/shard_map/pallas_call | solution.py:532
  99.9 9.6 %shard_map.146 = (bf16[2,8,4608]{2,1,0:T(8,128)(2,1)}, bf16[2,8,4608]{2,1,0:T(8,128)(2,1)}, bf16[3,2,8,4608]{3,2,1,0:T(8,128)(2,1)}, bf16[2,4608,512]{2,1,0:T(8,...) custom-call(bf16[2,8,4608]{2,1,0:T(8,128)(2,1)} %get-tuple-element.20.activ_ref, ...), custom_call_target="tpu_custom_call" | custom-call | tf_op jit(solution)/shard_map/pallas_call | solution.py:573

commit v2 on v1

--- a/solution.py
+++ b/solution.py
@@ -192,7 +192,7 @@
     read_ref,
     activ_ref,
     cotan_ref,
-    stash_out_ref,
+    stash_ref,
     normed_ref,
     down_ref,
     vals_ref,
@@ -202,19 +202,27 @@
     wo,
     xin,
     cot,
-    stash,
-    tgt,
+    staged,
+    landed,
+    peer_stash,
     psend,
     precv,
     moved,
     lhs,
+    scaled_own,
+    root_own,
+    gain_sum,
+    gain_send,
+    gain_recv,
     w_sem,
-    init_send,
-    init_recv,
     ex_send,
     ex_recv,
     sh_send,
     sh_recv,
+    st_send,
+    st_recv,
+    side_send,
+    side_recv,
 ):
     s = lax.axis_index("section")
     d = lax.axis_index("dp")
@@ -229,240 +237,335 @@
     features = wv.shape[2]
     slots = saved_ref.shape[0]
 
-    weight_copies = []
+    weight_copies = {}
     for group in range(2):
-        weight_copies.append(pltpu.make_async_copy(wv_hbm.at[group], wv.at[group], w_sem.at[group, 0]))
-        weight_copies.append(pltpu.make_async_copy(wo_hbm.at[group], wo.at[group], w_sem.at[group, 1]))
-    for copy in weight_copies:
-        copy.start()
+        for index, (source, target) in enumerate(((wv_hbm, wv), (wo_hbm, wo))):
+            weight_copies[group, index] = pltpu.make_async_copy(
+                source.at[group], target.at[group], w_sem.at[group, index]
+            )
+    for key in ((0, 0), (0, 1), (1, 1), (1, 0)):
+        weight_copies[key].start()
 
     barrier = pltpu.get_barrier_semaphore()
-    for target in ((s, peer), (after, d), (before, d)):
+    for target in ((s, peer), (after, d), (before, d), (after, peer), (before, peer)):
         pl.semaphore_signal(barrier, inc=1, device_id=target, device_id_type=MESH)
-    pl.semaphore_wait(barrier, 3)
-
-    def to_peer(src, dst, send, recv):
+
+    for group in range(2):
+        xin[0, group, 0] = arriving_ref[group]
+        cot[0, group, 0] = returning_ref[group]
+    for tick in range(1, ticks):
+        xin[tick, 2, 0] = fresh_ref[tick]
+    for group in range(2):
+        for index in range(slots - 1):
+            staged[index, group] = jnp.where(
+                fill_ref[group, 0] <= index, saved_ref[index + 1, group], saved_ref[index, group]
+            )
+    stash_ref[...] = saved_ref[...]
+    gain_sum[...] = jnp.zeros_like(gain_sum)
+    pl.semaphore_wait(barrier, 5)
+
+    def remote(src, dst, send, recv, target):
         return pltpu.make_async_remote_copy(
             src_ref=src, dst_ref=dst, send_sem=send, recv_sem=recv,
-            device_id=(s, peer), device_id_type=MESH,
-        )
-
-    def initial(index, src, dst):
-        return to_peer(src, dst, init_send.at[index], init_recv.at[index])
-
-    first_in = initial(0, arriving_ref, xin.at[0, pl.ds(0, 2), d])
-    first_cot = initial(1, returning_ref, cot.at[0, pl.ds(0, 2), d])
-    first_stash = initial(2, saved_ref, stash.at[:, :, d])
-    fresh_copy = initial(3, fresh_ref.at[pl.ds(1, ticks - 1)], xin.at[pl.ds(1, ticks - 1), 2, d])
-    target_copy = initial(4, targets_ref, tgt.at[:, d])
-    first_in.start()
-    first_cot.start()
-
-    @pl.when(s == 0)
-    def _():
-        fresh_copy.start()
-
-    @pl.when(s == sections - 1)
-    def _():
-        target_copy.start()
-
-    first_stash.start()
-    for group in range(2):
-        xin[0, group, d] = arriving_ref[group]
-        cot[0, group, d] = returning_ref[group]
-        for slot in range(slots):
-            stash[slot, group, d] = saved_ref[slot, group]
-    for tick in range(1, ticks):
-        xin[tick, 2, d] = fresh_ref[tick]
-    for tick in range(ticks):
-        tgt[tick, d] = targets_ref[tick]
-    gain_out_ref[...] = jnp.zeros_like(gain_out_ref)
+            device_id=target, device_id_type=MESH,
+        )
+
+    def initial(stream):
+        group = stream % 2
+        source, buffer = (arriving_ref, xin) if stream < 2 else (returning_ref, cot)
+        return remote(
+            source.at[group], buffer.at[0, group, 1],
+            sh_send.at[0, stream, 1], sh_recv.at[0, stream, 1], (s, peer),
+        )
+
+    def stash_copy(index, group):
+        return remote(
+            staged.at[index, group], landed.at[index, group],
+            st_send.at[index, group], st_recv.at[index, group], (s, peer),
+        )
+
+    fresh_copy = remote(
+        fresh_ref.at[pl.ds(1, ticks - 1)], xin.at[pl.ds(1, ticks - 1), 2, 1],
+        side_send.at[0], side_recv.at[0], (s, peer),
+    )
+    gain_copy = remote(gain_send, gain_recv, side_send.at[1], side_recv.at[1], (s, peer))
+    for stream in (0, 3, 1, 2):
+        initial(stream).start()
 
     def whole(block):
-        return block.astype(jnp.float32).reshape(rows, width)
+        return block.astype(jnp.float32).reshape(rows, block.shape[2])
 
     def parted(block):
-        return block.reshape(2, half, width).astype(jnp.bfloat16)
+        return block.reshape(2, half, block.shape[1]).astype(jnp.bfloat16)
 
     def exchange(tick, stream):
-        return to_peer(
-            psend.at[tick, stream], precv.at[tick, stream],
-            ex_send.at[tick, stream], ex_recv.at[tick, stream],
-        )
-
-    def shift(tick, stream):
+        return remote(
+            psend.at[tick, stream, 1], precv.at[tick, stream],
+            ex_send.at[tick, stream], ex_recv.at[tick, stream], (s, peer),
+        )
+
+    def shift(tick, stream, side):
         group = stream % 2
         if stream < 2:
             place, target, buffer = (group + is_last) % 2, after, xin
         else:
             place, target, buffer = (group + is_first) % 2, before, cot
-        return pltpu.make_async_remote_copy(
-            src_ref=moved.at[tick, stream], dst_ref=buffer.at[tick + 1, place],
-            send_sem=sh_send.at[tick, stream], recv_sem=sh_recv.at[tick + 1, stream - group + place],
-            device_id=(target, d), device_id_type=MESH,
-        )
-
-    def shift_arrival(tick, stream):
+        return remote(
+            moved.at[tick, stream], buffer.at[tick + 1, place, side],
+            sh_send.at[tick + 1, stream, side], sh_recv.at[tick + 1, stream - group + place, side],
+            (target, peer if side else d),
+        )
+
+    def finish_copy(tick):
+        return remote(
+            cot.at[tick + 1, 1, 0], cot.at[tick + 1, 1, 1],
+            sh_send.at[tick + 1, 1, 1], sh_recv.at[tick + 1, 3, 1], (s, peer),
+        )
+
+    def arrival(tick, stream, side):
         buffer = xin if stream < 2 else cot
-        return pltpu.make_async_remote_copy(
-            src_ref=moved.at[0, stream], dst_ref=buffer.at[tick, stream % 2],
-            send_sem=sh_send.at[0, stream], recv_sem=sh_recv.at[tick, stream],
-            device_id=(after, d), device_id_type=MESH,
-        )
-
-    def input_block(tick, group):
-        return whole(xin[tick, 2 * is_first if group == 0 else 1])
-
-    def cot_block(tick, group):
-        return whole(cot[tick, 0 if group == 0 else 1 + is_last])
+        return remote(
+            moved.at[0, stream], buffer.at[tick, stream % 2, side],
+            sh_send.at[tick, stream, side], sh_recv.at[tick, stream, side], (s, peer),
+        )
+
+    def arrive(tick, stream):
+        later = tick > 0
+        if stream == 0:
+            near, far = later & (s != 0), (tick == 0) | (s != 0)
+        elif stream == 3:
+            near, far = later & (s != sections - 1), None
+        else:
+            near, far = later, None
+
+        @pl.when(near)
+        def _():
+            arrival(tick, stream, 0).wait_recv()
+
+        if far is None:
+            arrival(tick, stream, 1).wait_recv()
+        else:
+            @pl.when(far)
+            def _():
+                arrival(tick, stream, 1).wait_recv()
+
+            @pl.when((tick == 1) & (s == 0))
+            def _():
+                fresh_copy.wait_recv()
+
+    def input_place(tick, group):
+        return 2 * is_first * jnp.minimum(tick, 1) if group == 0 else 1
 
     def norm_parts(values, group):
         inv_root = lax.rsqrt(jnp.mean(values * values, axis=-1, keepdims=True) + epsilon)
         scaled = values * inv_root
         return scaled, inv_root, (scaled * gain_ref[pl.ds(group, 1), :]).astype(jnp.bfloat16)
 
-    def value_product(rows_of, group):
-        return contract_sum(
+    def weights_ready(tick, key):
+        @pl.when(tick == 0)
+        def _():
+            weight_copies[key].wait()
+
+    def side_sends(tick, stream):
+        group, index = stream % 2, stream // 2
+
+        @pl.when(tick == 0)
+        def _():
+            for part in range(index, slots - 1, 2):
+                stash_copy(part, group).start()
+
+        if stream == 3:
+            @pl.when((tick == 0) & (s == 0))
+            def _():
+                fresh_copy.start()
+
+    def forward_start(tick, group):
+        arrive(tick, group)
+        lhs[...] = norm_parts(whole(xin[tick, input_place(tick, group)]), group)[2]
+        if group == 0:
+            weights_ready(tick, (0, 0))
+        values = contract_sum(
             width,
-            lambda at: jnp.dot(rows_of(at), wv[group, at, :], preferred_element_type=jnp.float32),
+            lambda at: jnp.dot(lhs[:, at], wv[group, at, :], preferred_element_type=jnp.float32),
             (rows, features),
         ).astype(jnp.bfloat16)
-
-    def arrive(tick, stream):
-        @pl.when(tick > 0)
-        def _():
-            shift_arrival(tick, stream).wait_recv()
-
-    def weights_ready(tick, index):
-        @pl.when(tick == 0)
-        def _():
-            weight_copies[index].wait()
-
-    def forward_start(tick, group):
-        arrive(tick, group)
-        lhs[...] = norm_parts(input_block(tick, group), group)[2]
-        weights_ready(tick, 2 * group)
-        values = value_product(lambda at: lhs[:, at], group)
-        weights_ready(tick, 2 * group + 1)
+        if group == 0:
+            weights_ready(tick, (0, 1))
 
         def step(at):
-            psend[tick, group, :, at] = jnp.dot(
-                values, wo[group, :, at], preferred_element_type=jnp.float32
-            ).astype(jnp.bfloat16)
+            psend[tick, group, :, :, at] = parted(
+                jnp.dot(values, wo[group, :, at], preferred_element_type=jnp.float32)
+            )
 
         chunk_loop(width, step)
         exchange(tick, group).start()
-
-    def send_on(tick, stream):
-        @pl.when(tick < ticks - 1)
-        def _():
-            shift(tick, stream).start()
+        side_sends(tick, group)
 
     def peer_sum(tick, stream):
         exchange(tick, stream).wait_recv()
-        return psend[tick, stream].astype(jnp.float32) + precv[tick, stream].astype(jnp.float32)
+        return psend[tick, stream, 0].astype(jnp.float32) + precv[tick, stream].astype(jnp.float32)
 
     def forward_finish(tick, group):
-        outputs = parted(input_block(tick, group) + peer_sum(tick, group))
+        own = xin[tick, input_place(tick, group), 0].astype(jnp.float32)
+        outputs = (own + peer_sum(tick, group)).astype(jnp.bfloat16)
         moved[tick, group] = outputs
-        send_on(tick, group)
+        going = tick < ticks - 1
+
+        @pl.when(going if group == 0 else going & (s != sections - 1))
+        def _():
+            shift(tick, group, 1).start()
+            shift(tick, group, 0).start()
+
         if group == 1:
-            @pl.when((tick < ticks - 1) & (s == sections - 1))
+            @pl.when(going & (s == sections - 1))
             def _():
-                cot[tick + 1, 2] = (
-                    outputs.astype(jnp.float32) - tgt[tick].astype(jnp.float32)
+                cot[tick + 1, 1, 0] = (
+                    outputs.astype(jnp.float32) - targets_ref[tick].astype(jnp.float32)
                 ).astype(jnp.bfloat16)
+                finish_copy(tick).start()
 
     def backward_start(tick, group):
         arrive(tick, 2 + group)
-        up_ref[group, tick] = cot_block(tick, group).astype(jnp.bfloat16)
+        up_ref[group, tick] = whole(cot[tick, group]).astype(jnp.bfloat16)
+        if group == 1:
+            weights_ready(tick, (1, 1))
         down = contract_sum(
             width,
             lambda at: times_transposed(up_ref[group, tick, :, at], wo[group, :, at]),
             (rows, features),
         ).astype(jnp.bfloat16)
         down_ref[group, tick] = down
+        if group == 1:
+            weights_ready(tick, (1, 0))
 
         def step(at):
-            psend[tick, 2 + group, :, at] = times_transposed(down, wv[group, at, :]).astype(
-                jnp.bfloat16
-            )
+            psend[tick, 2 + group, :, :, at] = parted(times_transposed(down, wv[group, at, :]))
 
         chunk_loop(width, step)
         exchange(tick, 2 + group).start()
-
-    def stash_step(tick, group):
-        block = xin[tick, 2 * is_first if group == 0 else 1]
+        side_sends(tick, 2 + group)
+
+    def own_source(tick, group):
+        block = xin[tick, input_place(tick, group), 0]
         for slot in range(slots):
-            stash[slot, group] = jnp.where(fill_ref[group, tick] == slot, block, stash[slot, group])
-
-    def source_values(tick, group):
-        normed_ref[group, tick] = norm_parts(whole(stash[read_ref[group, tick], group]), group)[2]
-        vals_ref[group, tick] = value_product(lambda at: normed_ref[group, tick, :, at], group)
+            stash_ref[slot, group] = jnp.where(fill_ref[group, tick] == slot, block, stash_ref[slot, group])
+        source = stash_ref[read_ref[group, tick], group].astype(jnp.float32)
+        scaled, inv_root, normed = norm_parts(source, group)
+        normed_ref[group, tick, 0] = normed
+        scaled_own[group] = scaled
+        root_own[group] = jnp.broadcast_to(inv_root, root_own.shape[1:])
+        gain_sum[group] += psend[tick, 2 + group, 0].astype(jnp.float32) * scaled
+
+    def peer_source(tick, group):
+        @pl.when(tick == 0)
+        def _():
+            filled = fill_ref[group, 0]
+            for index in range(slots - 1):
+                stash_copy(index, group).wait_recv()
+            for slot in range(slots):
+                low, high = max(slot - 1, 0), min(slot, slots - 2)
+                peer_stash[slot, group] = jnp.where(filled < slot, landed[low, group], landed[high, group])
+
+        block = xin[tick, input_place(tick, group), 1]
+        for slot in range(slots):
+            peer_stash[slot, group] = jnp.where(
+                fill_ref[group, tick] == slot, block, peer_stash[slot, group]
+            )
+        source = peer_stash[read_ref[group, tick], group].astype(jnp.float32)
+        scaled, _, normed = norm_parts(source, group)
+        normed_ref[group, tick, 1] = normed
+        gain_sum[group] += psend[tick, 2 + group, 1].astype(jnp.float32) * scaled
 
     def backward_finish(tick, group):
-        scaled, inv_root, _ = norm_parts(whole(stash[read_ref[group, tick], group]), group)
+        scaled = scaled_own[group]
         pulled = peer_sum(tick, 2 + group)
         weighted = pulled * gain_ref[pl.ds(group, 1), :]
         inner_mean = jnp.mean(weighted * scaled, axis=-1, keepdims=True)
-        moved[tick, 2 + group] = parted(
-            cot_block(tick, group) + inv_root * (weighted - scaled * inner_mean)
-        )
-        send_on(tick, 2 + group)
-        gain_out_ref[pl.ds(group, 1), :] += jnp.sum(pulled * scaled, axis=0, keepdims=True)
-
-    first_in.wait_recv()
-    xin[0, 2] = xin[0, 0]
+        moved[tick, 2 + group] = (
+            cot[tick, group, 0].astype(jnp.float32)
+            + root_own[group][:, :1] * (weighted - scaled * inner_mean)
+        ).astype(jnp.bfloat16)
+        going = tick < ticks - 1
+
+        @pl.when(going if group == 1 else going & (s != 0))
+        def _():
+            shift(tick, 2 + group, 1).start()
+            shift(tick, 2 + group, 0).start()
+
+    def tick_step(tick, _):
+        forward_start(tick, 0)
+        backward_start(tick, 1)
+
+        @pl.when(tick > 0)
+        def _():
+            backward_finish(tick - 1, 0)
+            peer_source(tick - 1, 1)
+
+        forward_finish(tick, 0)
+        forward_start(tick, 1)
+
+        @pl.when(tick > 0)
+        def _():
+            peer_source(tick - 1, 0)
+
+        own_source(tick, 1)
+        backward_finish(tick, 1)
+        backward_start(tick, 0)
+        own_source(tick, 0)
+        forward_finish(tick, 1)
+        return None
+
+    lax.fori_loop(0, ticks, tick_step, None)
+
+    for group in (1, 0):
+        peer_source(ticks - 1, group)
+        gain_send[pl.ds(group, 1), :] = jnp.sum(gain_sum[group], axis=0, keepdims=True)
+    gain_copy.start()
+    for group in range(2):
+        def chunk_values(at):
+            block = normed_ref[group, :, :, :, at].astype(jnp.float32)
+            left = block.reshape(ticks * rows, block.shape[3]).astype(jnp.bfloat16)
+            return jnp.dot(left, wv[group, at, :], preferred_element_type=jnp.float32)
+
+        vals_ref[group] = contract_sum(width, chunk_values, (ticks * rows, features)).astype(jnp.bfloat16)
+    backward_finish(ticks - 1, 0)
+    for group in range(2):
+        activ_ref[group] = moved[ticks - 1, group]
+        cotan_ref[group] = moved[ticks - 1, 2 + group]
+    gain_copy.wait()
+    gain_out_ref[...] = (gain_send[...] + gain_recv[...]) * (ticks * rows) ** (-0.5)
+
+    for stream in range(4):
+        initial(stream).wait_send()
+    for group in range(2):
+        for index in range(slots - 1):
+            stash_copy(index, group).wait_send()
 
     @pl.when(s == 0)
     def _():
-        fresh_copy.wait()
-
-    @pl.when(s == sections - 1)
-    def _():
-        target_copy.wait()
-
-    def tick_step(tick, _):
-        forward_start(tick, 0)
-        forward_start(tick, 1)
-        forward_finish(tick, 0)
-
-        @pl.when(tick == 0)
-        def _():
-            first_cot.wait_recv()
-            cot[0, 2] = cot[0, 1]
-
-        backward_start(tick, 0)
-        forward_finish(tick, 1)
-
-        @pl.when(tick == 0)
-        def _():
-            first_stash.wait_recv()
-
-        stash_step(tick, 0)
-        stash_step(tick, 1)
-        backward_start(tick, 1)
-        backward_finish(tick, 0)
-        source_values(tick, 0)
-        source_values(tick, 1)
-        backward_finish(tick, 1)
-        return None
-
-    lax.fori_loop(0, ticks, tick_step, None)
-
-    for group in range(2):
-        activ_ref[group] = moved[ticks - 1, group, d]
-        cotan_ref[group] = moved[ticks - 1, 2 + group, d]
-        for slot in range(slots):
-            stash_out_ref[slot, group] = stash[slot, group, d]
-    gain_out_ref[...] = gain_out_ref[...] * (ticks * rows) ** (-0.5)
-    for copy in (first_in, first_cot, first_stash):
-        copy.wait_send()
+        fresh_copy.wait_send()
+
     for tick in range(ticks):
         for stream in range(4):
             exchange(tick, stream).wait_send()
-            if tick < ticks - 1:
-                shift(tick, stream).wait_send()
+    for tick in range(ticks - 1):
+        for side in range(2):
+            shift(tick, 0, side).wait_send()
+            shift(tick, 3, side).wait_send()
+
+        @pl.when(s != sections - 1)
+        def _():
+            for side in range(2):
+                shift(tick, 1, side).wait_send()
+
+        @pl.when(s == sections - 1)
+        def _():
+            finish_copy(tick).wait_send()
+
+        @pl.when(s != 0)
+        def _():
+            for side in range(2):
+                shift(tick, 2, side).wait_send()
 
 
 def grads_kernel(
@@ -523,6 +626,11 @@
     ticks, half, width = fresh_rows.shape
     features = value_mats.shape[2]
     slots = saved.shape[0]
+    if slots < 2:
+        return body(
+            w_value, w_out, norm_gain, saved_inputs, arriving,
+            returning, fresh_rows, targets, fill_slots, read_slots,
+        )
     rows = 2 * half
     vmem = pl.BlockSpec(memory_space=pltpu.VMEM)
     smem = pl.BlockSpec(memory_space=pltpu.SMEM)
@@ -535,9 +643,9 @@
             shape(activations.shape, narrow),
             shape(cotangents.shape, narrow),
             shape(saved.shape, narrow),
-            shape((2, ticks, rows, width), narrow),
+            shape((2, ticks, 2, half, width), narrow),
             shape((2, ticks, rows, features), narrow),
-            shape((2, ticks, rows, features), narrow),
+            shape((2, ticks * rows, features), narrow),
             shape((2, ticks, rows, width), narrow),
             shape(gains.shape, jnp.float32),
         ),
@@ -547,20 +655,28 @@
             pltpu.VMEM(value_mats.shape, narrow),
             pltpu.VMEM(out_mats.shape, narrow),
             pltpu.VMEM((ticks, 3, 2, half, width), narrow),
-            pltpu.VMEM((ticks, 3, 2, half, width), narrow),
-            pltpu.VMEM((slots, 2, 2, half, width), narrow),
-            pltpu.VMEM((ticks, 2, half, width), narrow),
-            pltpu.VMEM((ticks, 4, rows, width), narrow),
-            pltpu.VMEM((ticks, 4, rows, width), narrow),
+            pltpu.VMEM((ticks, 2, 2, half, width), narrow),
+            pltpu.VMEM((slots - 1, 2, half, width), narrow),
+            pltpu.VMEM((slots - 1, 2, half, width), narrow),
+            pltpu.VMEM((slots, 2, half, width), narrow),
             pltpu.VMEM((ticks, 4, 2, half, width), narrow),
+            pltpu.VMEM((ticks, 4, half, width), narrow),
+            pltpu.VMEM((ticks, 4, half, width), narrow),
             pltpu.VMEM((rows, width), narrow),
+            pltpu.VMEM((2, half, width), jnp.float32),
+            pltpu.VMEM((2, half, 128), jnp.float32),
+            pltpu.VMEM((2, half, width), jnp.float32),
+            pltpu.VMEM((2, width), jnp.float32),
+            pltpu.VMEM((2, width), jnp.float32),
             pltpu.SemaphoreType.DMA((2, 2)),
-            pltpu.SemaphoreType.DMA((5,)),
-            pltpu.SemaphoreType.DMA((5,)),
             pltpu.SemaphoreType.DMA((ticks, 4)),
             pltpu.SemaphoreType.DMA((ticks, 4)),
-            pltpu.SemaphoreType.DMA((ticks, 4)),
-            pltpu.SemaphoreType.DMA((ticks, 4)),
+            pltpu.SemaphoreType.DMA((ticks, 4, 2)),
+            pltpu.SemaphoreType.DMA((ticks, 4, 2)),
+            pltpu.SemaphoreType.DMA((slots - 1, 2)),
+            pltpu.SemaphoreType.DMA((slots - 1, 2)),
+            pltpu.SemaphoreType.DMA((2,)),
+            pltpu.SemaphoreType.DMA((2,)),
         ],
         compiler_params=pltpu.CompilerParams(
             collective_id=0, has_side_effects=True, vmem_limit_bytes=VMEM_GRANT
@@ -569,7 +685,7 @@
         value_mats, out_mats, gains, saved, activations, cotangents,
         fresh_rows, targets, fill_slots[0].T, read_slots[0].T,
     )
-    flat = lambda block: block.reshape(2, ticks * rows, block.shape[3])
+    flat = lambda block: block.reshape(2, ticks * rows, block.shape[-1])
     grads = pl.pallas_call(
         functools.partial(grads_kernel, (ticks * rows) ** (-0.5)),
         out_shape=(

time: 110 us -> 84.8 us (0.77)
  Pallas kernels: 109 us -> 84 us
    pallas_call x1, Pallas kernels: 99.3 us -> 74.4 us  [relay_body(): pl.pallas_call(functools.partial(relay_kernel, sections), out_shape=(shap...]
where the time goes in v2:
time: 84.8 us; the launch traced here: 84.6 us
  Pallas kernels  84 us (99%)
    pallas_call x1, Pallas kernels, relay_body(): pl.pallas_call(functools.partial(relay_kernel, sections), out_shape=(shap...  74.4 us
    pallas_call x1, Pallas kernels, relay_body(): pl.pallas_call(functools.partial(grads_kernel, (ticks * rows) ** (-0.5)),...  9.63 us

profile of v2, /device:TPU:0, one launch (start us, length us, event | category | flops | bytes accessed | tf_op | source)
XLA Modules:
  0.0 84.6 jit_solution(5418228106495023863)
XLA Ops:
  0.6 74.4 %shard_map.145 = (bf16[2,8,4608]{2,1,0:T(8,128)(2,1)}, bf16[2,8,4608]{2,1,0:T(8,128)(2,1)}, bf16[3,2,8,4608]{3,2,1,0:T(8,128)(2,1)}, bf16[2,4,2,8,4608]{4,3,2,1,...) custom-call(bf16[2,4608,512]{2,1,0:T(8,128)(2,1)} %bitcast.21, ...), custom_call_target="tpu_custom_call" | custom-call | tf_op jit(solution)/shard_map/pallas_call | solution.py:640
  75.0 9.6 %shard_map.146 = (bf16[2,8,4608]{2,1,0:T(8,128)(2,1)}, bf16[2,8,4608]{2,1,0:T(8,128)(2,1)}, bf16[3,2,8,4608]{3,2,1,0:T(8,128)(2,1)}, bf16[2,4608,512]{2,1,0:T(8,...) custom-call(bf16[2,8,4608]{2,1,0:T(8,128)(2,1)} %get-tuple-element.20.activ_ref, ...), custom_call_target="tpu_custom_call" | custom-call | tf_op jit(solution)/shard_map/pallas_call | solution.py:689

commit v3 on v2

--- a/solution.py
+++ b/solution.py
@@ -183,21 +183,27 @@
     wv_hbm,
     wo_hbm,
     gain_ref,
-    saved_ref,
-    arriving_ref,
-    returning_ref,
-    fresh_ref,
-    targets_ref,
+    saved_hbm,
+    arriving_hbm,
+    returning_hbm,
+    fresh_hbm,
+    targets_hbm,
     fill_ref,
     read_ref,
-    activ_ref,
-    cotan_ref,
+    activ_hbm,
+    cotan_hbm,
+    stash_hbm,
+    normed_hbm,
+    down_hbm,
+    vals_hbm,
+    up_hbm,
+    gain_hbm,
     stash_ref,
     normed_ref,
     down_ref,
     vals_ref,
     up_ref,
-    gain_out_ref,
+    targets_ref,
     wv,
     wo,
     xin,
@@ -215,6 +221,8 @@
     gain_send,
     gain_recv,
     w_sem,
+    in_sem,
+    out_sem,
     ex_send,
     ex_recv,
     sh_send,
@@ -231,11 +239,25 @@
     before = lax.rem(s + sections - 1, sections)
     is_last = s // (sections - 1)
     is_first = before // (sections - 1)
-    ticks = fresh_ref.shape[0]
-    half, width = arriving_ref.shape[1:]
+    ticks = fresh_hbm.shape[0]
+    half, width = arriving_hbm.shape[1:]
     rows = 2 * half
     features = wv.shape[2]
-    slots = saved_ref.shape[0]
+    slots = saved_hbm.shape[0]
+
+    barrier = pltpu.get_barrier_semaphore()
+    for target in ((s, peer), (after, d), (before, d), (after, peer), (before, peer)):
+        pl.semaphore_signal(barrier, inc=1, device_id=target, device_id_type=MESH)
+
+    def take(index, source, target):
+        copy = pltpu.make_async_copy(source, target, in_sem.at[index])
+        copy.start()
+        return copy
+
+    own_blocks = {}
+    for stream in (0, 3, 1, 2):
+        source, buffer = (arriving_hbm, xin) if stream < 2 else (returning_hbm, cot)
+        own_blocks[stream] = take(stream, source.at[stream % 2], buffer.at[0, stream % 2, 0])
 
     weight_copies = {}
     for group in range(2):
@@ -246,21 +268,9 @@
     for key in ((0, 0), (0, 1), (1, 1), (1, 0)):
         weight_copies[key].start()
 
-    barrier = pltpu.get_barrier_semaphore()
-    for target in ((s, peer), (after, d), (before, d), (after, peer), (before, peer)):
-        pl.semaphore_signal(barrier, inc=1, device_id=target, device_id_type=MESH)
-
-    for group in range(2):
-        xin[0, group, 0] = arriving_ref[group]
-        cot[0, group, 0] = returning_ref[group]
-    for tick in range(1, ticks):
-        xin[tick, 2, 0] = fresh_ref[tick]
-    for group in range(2):
-        for index in range(slots - 1):
-            staged[index, group] = jnp.where(
-                fill_ref[group, 0] <= index, saved_ref[index + 1, group], saved_ref[index, group]
-            )
-    stash_ref[...] = saved_ref[...]
+    own_fresh = take(4, fresh_hbm.at[pl.ds(1, ticks - 1)], xin.at[pl.ds(1, ticks - 1), 2, 0])
+    own_targets = take(5, targets_hbm, targets_ref)
+    own_stash = take(6, saved_hbm, stash_ref)
     gain_sum[...] = jnp.zeros_like(gain_sum)
     pl.semaphore_wait(barrier, 5)
 
@@ -272,9 +282,9 @@
 
     def initial(stream):
         group = stream % 2
-        source, buffer = (arriving_ref, xin) if stream < 2 else (returning_ref, cot)
+        buffer = xin if stream < 2 else cot
         return remote(
-            source.at[group], buffer.at[0, group, 1],
+            buffer.at[0, group, 0], buffer.at[0, group, 1],
             sh_send.at[0, stream, 1], sh_recv.at[0, stream, 1], (s, peer),
         )
 
@@ -284,13 +294,18 @@
             st_send.at[index, group], st_recv.at[index, group], (s, peer),
         )
 
-    fresh_copy = remote(
-        fresh_ref.at[pl.ds(1, ticks - 1)], xin.at[pl.ds(1, ticks - 1), 2, 1],
-        side_send.at[0], side_recv.at[0], (s, peer),
-    )
-    gain_copy = remote(gain_send, gain_recv, side_send.at[1], side_recv.at[1], (s, peer))
+    def fresh_copy(tick):
+        return remote(
+            xin.at[tick, 2, 0], xin.at[tick, 2, 1],
+            side_send.at[tick], side_recv.at[tick], (s, peer),
+        )
+
+    gain_copy = remote(gain_send, gain_recv, side_send.at[0], side_recv.at[0], (s, peer))
     for stream in (0, 3, 1, 2):
+        own_blocks[stream].wait()
         initial(stream).start()
+    own_fresh.wait()
+    own_targets.wait()
 
     def whole(block):
         return block.astype(jnp.float32).reshape(rows, block.shape[2])
@@ -349,9 +364,9 @@
             def _():
                 arrival(tick, stream, 1).wait_recv()
 
-            @pl.when((tick == 1) & (s == 0))
+            @pl.when(later & (s == 0))
             def _():
-                fresh_copy.wait_recv()
+                fresh_copy(tick).wait_recv()
 
     def input_place(tick, group):
         return 2 * is_first * jnp.minimum(tick, 1) if group == 0 else 1
@@ -366,18 +381,14 @@
         def _():
             weight_copies[key].wait()
 
-    def side_sends(tick, stream):
-        group, index = stream % 2, stream // 2
-
-        @pl.when(tick == 0)
-        def _():
-            for part in range(index, slots - 1, 2):
-                stash_copy(part, group).start()
-
-        if stream == 3:
-            @pl.when((tick == 0) & (s == 0))
-            def _():
-                fresh_copy.start()
+    def stash_sends(tick, group):
+        @pl.when(tick == ticks - 1)
+        def _():
+            for index in range(slots - 1):
+                stash_copy(index, group).start()
+
+    def exchanged(tick, stream):
+        return (s != 0) | (tick == ticks - 1) if stream == 2 else tick >= 0
 
     def forward_start(tick, group):
         arrive(tick, group)
@@ -399,7 +410,6 @@
 
         chunk_loop(width, step)
         exchange(tick, group).start()
-        side_sends(tick, group)
 
     def peer_sum(tick, stream):
         exchange(tick, stream).wait_recv()
@@ -442,10 +452,26 @@
             psend[tick, 2 + group, :, :, at] = parted(times_transposed(down, wv[group, at, :]))
 
         chunk_loop(width, step)
-        exchange(tick, 2 + group).start()
-        side_sends(tick, 2 + group)
+
+        @pl.when(exchanged(tick, 2 + group))
+        def _():
+            exchange(tick, 2 + group).start()
+
+        if group == 0:
+            @pl.when((tick < ticks - 1) & (s == 0))
+            def _():
+                fresh_copy(tick + 1).start()
 
     def own_source(tick, group):
+        @pl.when(tick == 0)
+        def _():
+            if group == 1:
+                own_stash.wait()
+            for index in range(slots - 1):
+                staged[index, group] = jnp.where(
+                    fill_ref[group, 0] <= index, stash_ref[index + 1, group], stash_ref[index, group]
+                )
+
         block = xin[tick, input_place(tick, group), 0]
         for slot in range(slots):
             stash_ref[slot, group] = jnp.where(fill_ref[group, tick] == slot, block, stash_ref[slot, group])
@@ -456,16 +482,15 @@
         root_own[group] = jnp.broadcast_to(inv_root, root_own.shape[1:])
         gain_sum[group] += psend[tick, 2 + group, 0].astype(jnp.float32) * scaled
 
+    def peer_stash_start(group):
+        filled = fill_ref[group, 0]
+        for index in range(slots - 1):
+            stash_copy(index, group).wait_recv()
+        for slot in range(slots):
+            low, high = max(slot - 1, 0), min(slot, slots - 2)
+            peer_stash[slot, group] = jnp.where(filled < slot, landed[low, group], landed[high, group])
+
     def peer_source(tick, group):
-        @pl.when(tick == 0)
-        def _():
-            filled = fill_ref[group, 0]
-            for index in range(slots - 1):
-                stash_copy(index, group).wait_recv()
-            for slot in range(slots):
-                low, high = max(slot - 1, 0), min(slot, slots - 2)
-                peer_stash[slot, group] = jnp.where(filled < slot, landed[low, group], landed[high, group])
-
         block = xin[tick, input_place(tick, group), 1]
         for slot in range(slots):
             peer_stash[slot, group] = jnp.where(
@@ -476,7 +501,7 @@
         normed_ref[group, tick, 1] = normed
         gain_sum[group] += psend[tick, 2 + group, 1].astype(jnp.float32) * scaled
 
-    def backward_finish(tick, group):
+    def gradient(tick, group):
         scaled = scaled_own[group]
         pulled = peer_sum(tick, 2 + group)
         weighted = pulled * gain_ref[pl.ds(group, 1), :]
@@ -485,12 +510,16 @@
             cot[tick, group, 0].astype(jnp.float32)
             + root_own[group][:, :1] * (weighted - scaled * inner_mean)
         ).astype(jnp.bfloat16)
-        going = tick < ticks - 1
-
-        @pl.when(going if group == 1 else going & (s != 0))
-        def _():
-            shift(tick, 2 + group, 1).start()
-            shift(tick, 2 + group, 0).start()
+
+    def backward_finish(tick, group):
+        @pl.when(exchanged(tick, 2 + group))
+        def _():
+            gradient(tick, group)
+
+            @pl.when(tick < ticks - 1)
+            def _():
+                shift(tick, 2 + group, 1).start()
+                shift(tick, 2 + group, 0).start()
 
     def tick_step(tick, _):
         forward_start(tick, 0)
@@ -499,15 +528,11 @@
         @pl.when(tick > 0)
         def _():
             backward_finish(tick - 1, 0)
-            peer_source(tick - 1, 1)
-
+
+        stash_sends(tick, 1)
         forward_finish(tick, 0)
         forward_start(tick, 1)
-
-        @pl.when(tick > 0)
-        def _():
-            peer_source(tick - 1, 0)
-
+        stash_sends(tick, 0)
         own_source(tick, 1)
         backward_finish(tick, 1)
         backward_start(tick, 0)
@@ -517,8 +542,26 @@
 
     lax.fori_loop(0, ticks, tick_step, None)
 
+    def give(index, source, target):
+        copy = pltpu.make_async_copy(source, target, out_sem.at[index])
+        copy.start()
+        return copy
+
+    given = [
+        give(0, stash_ref, stash_hbm),
+        give(1, up_ref, up_hbm),
+        give(2, down_ref, down_hbm),
+        give(3, moved.at[ticks - 1, pl.ds(0, 2)], activ_hbm),
+    ]
     for group in (1, 0):
-        peer_source(ticks - 1, group)
+        peer_stash_start(group)
+
+        def source_step(tick, _):
+            peer_source(tick, group)
+            return None
+
+        lax.fori_loop(0, ticks, source_step, None)
+        given.append(give(4 + group, normed_ref.at[group], normed_hbm.at[group]))
         gain_send[pl.ds(group, 1), :] = jnp.sum(gain_sum[group], axis=0, keepdims=True)
     gain_copy.start()
     for group in range(2):
@@ -528,13 +571,16 @@
             return jnp.dot(left, wv[group, at, :], preferred_element_type=jnp.float32)
 
         vals_ref[group] = contract_sum(width, chunk_values, (ticks * rows, features)).astype(jnp.bfloat16)
+    given.append(give(6, vals_ref, vals_hbm))
     backward_finish(ticks - 1, 0)
-    for group in range(2):
-        activ_ref[group] = moved[ticks - 1, group]
-        cotan_ref[group] = moved[ticks - 1, 2 + group]
-    gain_copy.wait()
-    gain_out_ref[...] = (gain_send[...] + gain_recv[...]) * (ticks * rows) ** (-0.5)
-
+    given.append(give(7, moved.at[ticks - 1, pl.ds(2, 2)], cotan_hbm))
+    gain_copy.wait_recv()
+    gain_sum[0, pl.ds(0, 2), :] = (gain_send[...] + gain_recv[...]) * (ticks * rows) ** (-0.5)
+    given.append(give(8, gain_sum.at[0, pl.ds(0, 2)], gain_hbm))
+    for copy in given:
+        copy.wait()
+
+    gain_copy.wait_send()
     for stream in range(4):
         initial(stream).wait_send()
     for group in range(2):
@@ -543,11 +589,14 @@
 
     @pl.when(s == 0)
     def _():
-        fresh_copy.wait_send()
+        for tick in range(1, ticks):
+            fresh_copy(tick).wait_send()
 
     for tick in range(ticks):
         for stream in range(4):
-            exchange(tick, stream).wait_send()
+            @pl.when(exchanged(tick, stream))
+            def _():
+                exchange(tick, stream).wait_send()
     for tick in range(ticks - 1):
         for side in range(2):
             shift(tick, 0, side).wait_send()
@@ -649,9 +698,15 @@
             shape((2, ticks, rows, width), narrow),
             shape(gains.shape, jnp.float32),
         ),
-        in_specs=[hbm, hbm] + [vmem] * 6 + [smem] * 2,
-        out_specs=(vmem,) * 8,
+        in_specs=[hbm, hbm, vmem] + [hbm] * 5 + [smem] * 2,
+        out_specs=(hbm,) * 8,
         scratch_shapes=[
+            pltpu.VMEM(saved.shape, narrow),
+            pltpu.VMEM((2, ticks, 2, half, width), narrow),
+            pltpu.VMEM((2, ticks, rows, features), narrow),
+            pltpu.VMEM((2, ticks * rows, features), narrow),
+            pltpu.VMEM((2, ticks, rows, width), narrow),
+            pltpu.VMEM((ticks, half, width), narrow),
             pltpu.VMEM(value_mats.shape, narrow),
             pltpu.VMEM(out_mats.shape, narrow),
             pltpu.VMEM((ticks, 3, 2, half, width), narrow),
@@ -669,14 +724,16 @@
             pltpu.VMEM((2, width), jnp.float32),
             pltpu.VMEM((2, width), jnp.float32),
             pltpu.SemaphoreType.DMA((2, 2)),
+            pltpu.SemaphoreType.DMA((7,)),
+            pltpu.SemaphoreType.DMA((9,)),
             pltpu.SemaphoreType.DMA((ticks, 4)),
             pltpu.SemaphoreType.DMA((ticks, 4)),
             pltpu.SemaphoreType.DMA((ticks, 4, 2)),
             pltpu.SemaphoreType.DMA((ticks, 4, 2)),
             pltpu.SemaphoreType.DMA((slots - 1, 2)),
             pltpu.SemaphoreType.DMA((slots - 1, 2)),
-            pltpu.SemaphoreType.DMA((2,)),
-            pltpu.SemaphoreType.DMA((2,)),
+            pltpu.SemaphoreType.DMA((ticks,)),
+            pltpu.SemaphoreType.DMA((ticks,)),
         ],
         compiler_params=pltpu.CompilerParams(
             collective_id=0, has_side_effects=True, vmem_limit_bytes=VMEM_GRANT

time: 84.8 us -> 86.2 us (1.017)
  Pallas kernels: 84 us -> 85.3 us
    pallas_call x1, Pallas kernels: 74.4 us -> 75.7 us  [relay_body(): pl.pallas_call(functools.partial(relay_kernel, sections), out_shape=(shap...]
where the time goes in v3:
time: 86.2 us; the launch traced here: 86 us
  Pallas kernels  85.3 us (99%)
    pallas_call x1, Pallas kernels, relay_body(): pl.pallas_call(functools.partial(relay_kernel, sections), out_shape=(shap...  75.7 us
    pallas_call x1, Pallas kernels, relay_body(): pl.pallas_call(functools.partial(grads_kernel, (ticks * rows) ** (-0.5)),...  9.63 us

profile of v3, /device:TPU:0, one launch (start us, length us, event | category | flops | bytes accessed | tf_op | source)
XLA Modules:
  0.0 86.0 jit_solution(11197492790079874183)
XLA Ops:
  0.6 75.7 %shard_map.145 = (bf16[2,8,4608]{2,1,0:T(8,128)(2,1)}, bf16[2,8,4608]{2,1,0:T(8,128)(2,1)}, bf16[3,2,8,4608]{3,2,1,0:T(8,128)(2,1)}, bf16[2,4,2,8,4608]{4,3,2,1,...) custom-call(bf16[2,4608,512]{2,1,0:T(8,128)(2,1)} %bitcast.21, ...), custom_call_target="tpu_custom_call" | custom-call | tf_op jit(solution)/shard_map/pallas_call | solution.py:689
  76.3 9.6 %shard_map.146 = (bf16[2,8,4608]{2,1,0:T(8,128)(2,1)}, bf16[2,8,4608]{2,1,0:T(8,128)(2,1)}, bf16[3,2,8,4608]{3,2,1,0:T(8,128)(2,1)}, bf16[2,4608,512]{2,1,0:T(8,...) custom-call(bf16[2,8,4608]{2,1,0:T(8,128)(2,1)} %get-tuple-element.20.activ_ref, ...), custom_call_target="tpu_custom_call" | custom-call | tf_op jit(solution)/shard_map/pallas_call | solution.py:746

commit v4 on v3

--- a/solution.py
+++ b/solution.py
@@ -178,6 +178,14 @@
     return lax.fori_loop(0, width // size, step, jnp.zeros(shape, jnp.float32), unroll=UNROLL)
 
 
+def input_gradient(pulled, cotangent, scaled, root, gain_row):
+    weighted = pulled * gain_row
+    inner_mean = jnp.mean(weighted * scaled, axis=-1, keepdims=True)
+    return (
+        cotangent.astype(jnp.float32) + root[:, :1] * (weighted - scaled * inner_mean)
+    ).astype(jnp.bfloat16)
+
+
 def relay_kernel(
     sections,
     wv_hbm,
@@ -190,8 +198,12 @@
     targets_hbm,
     fill_ref,
     read_ref,
-    activ_hbm,
-    cotan_hbm,
+    part_own_hbm,
+    part_peer_hbm,
+    input_hbm,
+    cot_hbm,
+    scaled_hbm,
+    root_hbm,
     stash_hbm,
     normed_hbm,
     down_hbm,
@@ -388,7 +400,8 @@
                 stash_copy(index, group).start()
 
     def exchanged(tick, stream):
-        return (s != 0) | (tick == ticks - 1) if stream == 2 else tick >= 0
+        going = tick < ticks - 1
+        return going & (s != 0) if stream == 2 else going
 
     def forward_start(tick, group):
         arrive(tick, group)
@@ -409,30 +422,37 @@
             )
 
         chunk_loop(width, step)
-        exchange(tick, group).start()
+
+        @pl.when(exchanged(tick, group))
+        def _():
+            exchange(tick, group).start()
 
     def peer_sum(tick, stream):
         exchange(tick, stream).wait_recv()
         return psend[tick, stream, 0].astype(jnp.float32) + precv[tick, stream].astype(jnp.float32)
 
     def forward_finish(tick, group):
-        own = xin[tick, input_place(tick, group), 0].astype(jnp.float32)
-        outputs = (own + peer_sum(tick, group)).astype(jnp.bfloat16)
-        moved[tick, group] = outputs
-        going = tick < ticks - 1
-
-        @pl.when(going if group == 0 else going & (s != sections - 1))
-        def _():
-            shift(tick, group, 1).start()
-            shift(tick, group, 0).start()
-
-        if group == 1:
-            @pl.when(going & (s == sections - 1))
-            def _():
-                cot[tick + 1, 1, 0] = (
-                    outputs.astype(jnp.float32) - targets_ref[tick].astype(jnp.float32)
-                ).astype(jnp.bfloat16)
-                finish_copy(tick).start()
+        @pl.when(exchanged(tick, group))
+        def _():
+            own = xin[tick, input_place(tick, group), 0].astype(jnp.float32)
+            outputs = (own + peer_sum(tick, group)).astype(jnp.bfloat16)
+            moved[tick, group] = outputs
+
+            def send_on():
+                shift(tick, group, 1).start()
+                shift(tick, group, 0).start()
+
+            if group == 0:
+                send_on()
+            else:
+                pl.when(s != sections - 1)(send_on)
+
+                @pl.when(s == sections - 1)
+                def _():
+                    cot[tick + 1, 1, 0] = (
+                        outputs.astype(jnp.float32) - targets_ref[tick].astype(jnp.float32)
+                    ).astype(jnp.bfloat16)
+                    finish_copy(tick).start()
 
     def backward_start(tick, group):
         arrive(tick, 2 + group)
@@ -501,25 +521,15 @@
         normed_ref[group, tick, 1] = normed
         gain_sum[group] += psend[tick, 2 + group, 1].astype(jnp.float32) * scaled
 
-    def gradient(tick, group):
-        scaled = scaled_own[group]
-        pulled = peer_sum(tick, 2 + group)
-        weighted = pulled * gain_ref[pl.ds(group, 1), :]
-        inner_mean = jnp.mean(weighted * scaled, axis=-1, keepdims=True)
-        moved[tick, 2 + group] = (
-            cot[tick, group, 0].astype(jnp.float32)
-            + root_own[group][:, :1] * (weighted - scaled * inner_mean)
-        ).astype(jnp.bfloat16)
-
     def backward_finish(tick, group):
         @pl.when(exchanged(tick, 2 + group))
         def _():
-            gradient(tick, group)
-
-            @pl.when(tick < ticks - 1)
-            def _():
-                shift(tick, 2 + group, 1).start()
-                shift(tick, 2 + group, 0).start()
+            pulled = peer_sum(tick, 2 + group)
+            moved[tick, 2 + group] = input_gradient(
+                pulled, cot[tick, group, 0], scaled_own[group], root_own[group], gain_ref[pl.ds(group, 1), :]
+            )
+            shift(tick, 2 + group, 1).start()
+            shift(tick, 2 + group, 0).start()
 
     def tick_step(tick, _):
         forward_start(tick, 0)
@@ -547,11 +557,18 @@
         copy.start()
         return copy
 
+    last = ticks - 1
     given = [
-        give(0, stash_ref, stash_hbm),
-        give(1, up_ref, up_hbm),
-        give(2, down_ref, down_hbm),
-        give(3, moved.at[ticks - 1, pl.ds(0, 2)], activ_hbm),
+        give(0, psend.at[last, :, 0], part_own_hbm),
+        give(1, psend.at[last, :, 1], part_peer_hbm),
+        give(2, xin.at[last, input_place(last, 0), 0], input_hbm.at[0]),
+        give(3, xin.at[last, 1, 0], input_hbm.at[1]),
+        give(4, cot.at[last, :, 0], cot_hbm),
+        give(5, scaled_own, scaled_hbm),
+        give(6, root_own, root_hbm),
+        give(7, stash_ref, stash_hbm),
+        give(8, up_ref, up_hbm),
+        give(9, down_ref, down_hbm),
     ]
     for group in (1, 0):
         peer_stash_start(group)
@@ -561,7 +578,7 @@
             return None
 
         lax.fori_loop(0, ticks, source_step, None)
-        given.append(give(4 + group, normed_ref.at[group], normed_hbm.at[group]))
+        given.append(give(10 + group, normed_ref.at[group], normed_hbm.at[group]))
         gain_send[pl.ds(group, 1), :] = jnp.sum(gain_sum[group], axis=0, keepdims=True)
     gain_copy.start()
     for group in range(2):
@@ -571,12 +588,10 @@
             return jnp.dot(left, wv[group, at, :], preferred_element_type=jnp.float32)
 
         vals_ref[group] = contract_sum(width, chunk_values, (ticks * rows, features)).astype(jnp.bfloat16)
-    given.append(give(6, vals_ref, vals_hbm))
-    backward_finish(ticks - 1, 0)
-    given.append(give(7, moved.at[ticks - 1, pl.ds(2, 2)], cotan_hbm))
+    given.append(give(12, vals_ref, vals_hbm))
     gain_copy.wait_recv()
     gain_sum[0, pl.ds(0, 2), :] = (gain_send[...] + gain_recv[...]) * (ticks * rows) ** (-0.5)
-    given.append(give(8, gain_sum.at[0, pl.ds(0, 2)], gain_hbm))
+    given.append(give(13, gain_sum.at[0, pl.ds(0, 2)], gain_hbm))
     for copy in given:
         copy.wait()
 
@@ -618,43 +633,82 @@
 
 
 def grads_kernel(
-    grad_scale, activ_ref, cotan_ref, stash_ref, gain_ref, normed_ref, down_ref, vals_ref, up_ref,
-    activ_hbm, cotan_hbm, stash_hbm, value_hbm, out_hbm, gain_hbm,
-    value_grad, out_grad, small_sem, grad_sem,
+    grad_scale, stash_in, gain_in, normed_in, down_in, vals_in, up_in,
+    stash_hbm, value_hbm, out_hbm, gain_hbm,
+    stash, gain, normed, down, vals, up, value_grad, out_grad,
+    load_sem, chunk_sem, small_sem, grad_sem,
 ):
-    small = [
-        pltpu.make_async_copy(source, target, small_sem.at[index])
+    width = normed.shape[2]
+    size = CHUNK if width % CHUNK == 0 else width
+    count = width // size
+    loads = [
+        pltpu.make_async_copy(source, target, load_sem.at[index])
         for index, (source, target) in enumerate(
-            ((activ_ref, activ_hbm), (cotan_ref, cotan_hbm), (stash_ref, stash_hbm), (gain_ref, gain_hbm))
+            ((down_in, down), (vals_in, vals), (stash_in, stash), (gain_in, gain))
         )
     ]
-    for copy in small:
+
+    def place(index):
+        return pl.ds(pl.multiple_of(index * size, size), size)
+
+    def chunks(index):
+        at = place(index)
+        return [
+            pltpu.make_async_copy(source.at[:, :, at], target.at[:, :, at], chunk_sem.at[index, side])
+            for side, (source, target) in enumerate(((normed_in, normed), (up_in, up)))
+        ]
+
+    for copy in loads[:2]:
         copy.start()
-    width = normed_ref.shape[2]
-    size = CHUNK if width % CHUNK == 0 else width
+    for index in range(count):
+        for copy in chunks(index):
+            copy.start()
+    for copy in loads[2:]:
+        copy.start()
+    for copy in loads[:2]:
+        copy.wait()
 
     def step(index, _):
-        at = pl.ds(pl.multiple_of(index * size, size), size)
+        at = place(index)
+        for copy in chunks(index):
+            copy.wait()
         for group in range(2):
             value_grad[group, at, :] = (
-                transposed_times(normed_ref[group, :, at], down_ref[group]) * grad_scale
+                transposed_times(normed[group, :, at], down[group]) * grad_scale
             ).astype(jnp.bfloat16)
             pltpu.make_async_copy(
                 value_grad.at[group, at, :], value_hbm.at[group, at, :], grad_sem.at[0]
             ).start()
             out_grad[group, :, at] = (
-                transposed_times(vals_ref[group], up_ref[group, :, at]) * grad_scale
+                transposed_times(vals[group], up[group, :, at]) * grad_scale
             ).astype(jnp.bfloat16)
             pltpu.make_async_copy(
                 out_grad.at[group, :, at], out_hbm.at[group, :, at], grad_sem.at[1]
             ).start()
         return None
 
-    lax.fori_loop(0, width // size, step, None)
+    lax.fori_loop(0, count, step, None)
+    small = [
+        pltpu.make_async_copy(stash, stash_hbm, small_sem.at[0]),
+        pltpu.make_async_copy(gain, gain_hbm, small_sem.at[1]),
+    ]
+    for load, copy in zip(loads[2:], small):
+        load.wait()
+        copy.start()
     pltpu.make_async_copy(value_grad, value_hbm, grad_sem.at[0]).wait()
     pltpu.make_async_copy(out_grad, out_hbm, grad_sem.at[1]).wait()
     for copy in small:
         copy.wait()
+
+
+def final_kernel(own_ref, sent_ref, input_ref, cot_ref, scaled_ref, root_ref, gain_ref, activ_ref, cotan_ref):
+    for group in range(2):
+        total = own_ref[group].astype(jnp.float32) + sent_ref[group].astype(jnp.float32)
+        activ_ref[group] = (input_ref[group].astype(jnp.float32) + total).astype(jnp.bfloat16)
+        pulled = own_ref[2 + group].astype(jnp.float32) + sent_ref[2 + group].astype(jnp.float32)
+        cotan_ref[group] = input_gradient(
+            pulled, cot_ref[group], scaled_ref[group], root_ref[group], gain_ref[pl.ds(group, 1), :]
+        )
 
 
 def relay_body(
@@ -686,11 +740,19 @@
     hbm = pl.BlockSpec(memory_space=pl.ANY)
     shape = jax.ShapeDtypeStruct
     narrow = jnp.bfloat16
-    final_rows, gradients, stash_rows, normed, down, values, upstream, gain_sums = pl.pallas_call(
+    part_shape = shape((4, half, width), narrow)
+    (
+        part_own, part_peer, inputs, last_cot, scaled, root,
+        stash_rows, normed, down, values, upstream, gain_sums,
+    ) = pl.pallas_call(
         functools.partial(relay_kernel, sections),
         out_shape=(
+            part_shape,
+            part_shape,
             shape(activations.shape, narrow),
             shape(cotangents.shape, narrow),
+            shape((2, half, width), jnp.float32),
+            shape((2, half, 128), jnp.float32),
             shape(saved.shape, narrow),
             shape((2, ticks, 2, half, width), narrow),
             shape((2, ticks, rows, features), narrow),
@@ -699,7 +761,7 @@
             shape(gains.shape, jnp.float32),
         ),
         in_specs=[hbm, hbm, vmem] + [hbm] * 5 + [smem] * 2,
-        out_specs=(hbm,) * 8,
+        out_specs=(hbm,) * 12,
         scratch_shapes=[
             pltpu.VMEM(saved.shape, narrow),
             pltpu.VMEM((2, ticks, 2, half, width), narrow),
@@ -725,7 +787,7 @@
             pltpu.VMEM((2, width), jnp.float32),
             pltpu.SemaphoreType.DMA((2, 2)),
             pltpu.SemaphoreType.DMA((7,)),
-            pltpu.SemaphoreType.DMA((9,)),
+            pltpu.SemaphoreType.DMA((14,)),
             pltpu.SemaphoreType.DMA((ticks, 4)),
             pltpu.SemaphoreType.DMA((ticks, 4)),
             pltpu.SemaphoreType.DMA((ticks, 4, 2)),
@@ -742,28 +804,40 @@
         value_mats, out_mats, gains, saved, activations, cotangents,
         fresh_rows, targets, fill_slots[0].T, read_slots[0].T,
     )
+    part_sent = shifted(part_peer, "dp", 1)
     flat = lambda block: block.reshape(2, ticks * rows, block.shape[-1])
-    grads = pl.pallas_call(
+    operands = (stash_rows, gain_sums, flat(normed), flat(down), values, flat(upstream))
+    stash_out, value_grad, out_grad, gain_grad = pl.pallas_call(
         functools.partial(grads_kernel, (ticks * rows) ** (-0.5)),
         out_shape=(
-            shape(activations.shape, narrow),
-            shape(cotangents.shape, narrow),
             shape(saved.shape, narrow),
             shape(value_mats.shape, narrow),
             shape(out_mats.shape, narrow),
             shape(gains.shape, jnp.float32),
         ),
-        in_specs=[vmem] * 8,
-        out_specs=(hbm,) * 6,
-        scratch_shapes=[
+        in_specs=[hbm] * 6,
+        out_specs=(hbm,) * 4,
+        scratch_shapes=[pltpu.VMEM(block.shape, block.dtype) for block in operands] + [
             pltpu.VMEM(value_mats.shape, narrow),
             pltpu.VMEM(out_mats.shape, narrow),
             pltpu.SemaphoreType.DMA((4,)),
+            pltpu.SemaphoreType.DMA((width // CHUNK if width % CHUNK == 0 else 1, 2)),
+            pltpu.SemaphoreType.DMA((2,)),
             pltpu.SemaphoreType.DMA((2,)),
         ],
         compiler_params=pltpu.CompilerParams(vmem_limit_bytes=VMEM_GRANT),
-    )(final_rows, gradients, stash_rows, gain_sums, flat(normed), flat(down), flat(values), flat(upstream))
-    return tuple(block[None] for block in grads)
+        cost_estimate=pl.CostEstimate(
+            flops=32 * ticks * rows * width * features, bytes_accessed=8 * width * features, transcendentals=0
+        ),
+    )(*operands)
+    final_rows, gradients = pl.pallas_call(
+        final_kernel,
+        out_shape=(shape(activations.shape, narrow), shape(cotangents.shape, narrow)),
+        in_specs=[vmem] * 7,
+        out_specs=(vmem,) * 2,
+    )(part_own, part_sent, inputs, last_cot, scaled, root, gains)
+    results = (final_rows, gradients, stash_out, value_grad, out_grad, gain_grad)
+    return tuple(block[None] for block in results)
 
 
 def solution(mesh):

time: 86.2 us -> 86.7 us (level)
    pallas_call x1 -> x2, Pallas kernels: 75.7 us -> 74.9 us  [the longest x1 72.8 us: relay_body(): pl.pallas_call(functools.partial(relay_kernel, sections), out_shape=(part...]
  transfers between devices with their start and end apart: 0 -> 1, of which waited for: 0 -> 0; matrix products, arithmetic and copies ran while one was open for 0% -> 0% of each run, Pallas kernels for 0% -> 11%
where the time goes in v4:
time: 86.7 us; the launch traced here: 86.4 us
  Pallas kernels  84.5 us (97%)
    pallas_call x1, Pallas kernels, relay_body(): pl.pallas_call(functools.partial(relay_kernel, sections), out_shape=(part...  72.8 us
    pallas_call x1, Pallas kernels, relay_body(): pl.pallas_call(functools.partial(grads_kernel, (ticks * rows) ** (-0.5)),...  9.53 us
    pallas_call x1, Pallas kernels, relay_body(): pl.pallas_call(final_kernel, out_shape=(shape(activations.shape, narrow),...  2.16 us
  transfers between devices with their start and end apart: 1, of which 0 were waited for; matrix products, arithmetic and copies ran while one was open for 0% of the time, Pallas kernels for 11%

profile of v4, /device:TPU:0, one launch (start us, length us, event | category | flops | bytes accessed | tf_op | source)
XLA Modules:
  0.0 86.4 jit_solution(890972931945653577)
XLA Ops:
  0.6 72.8 %shard_map.145 = (bf16[4,8,4608]{2,1,0:T(8,128)(2,1)}, bf16[4,8,4608]{2,1,0:T(8,128)(2,1)}, bf16[2,8,4608]{2,1,0:T(8,128)(2,1)}, bf16[2,8,4608]{2,1,0:T(8,128)(2...) custom-call(bf16[2,4608,512]{2,1,0:T(8,128)(2,1)} %bitcast.21, ...), custom_call_target="tpu_custom_call" | custom-call | tf_op jit(solution)/shard_map/pallas_call | solution.py:747
  73.4 0.6 collective-permute-start
  74.0 9.5 %shard_map.147 = (bf16[3,2,8,4608]{3,2,1,0:T(8,128)(2,1)}, bf16[2,4608,512]{2,1,0:T(8,128)(2,1)}, bf16[2,512,4608]{2,1,0:T(8,128)(2,1)}, f32[2,4608]{1,0:T(2,128)}) custom-call(bf16[3,2,8,4608]{3,2,1,0:T(8,128)(2,1)} %get-tuple-element.32.stash_in, f32[2,4608]{1,0:T(2,128)} %get-tuple-element.33.gain_in, bf16[2,64,4608]{2,1,0:T(8,128)(2,1)} %bitcast.30, ...), custom_call_target="tpu_custom_call" | custom-call | flops 4831838208 | bytes 18874368 | tf_op jit(solution)/shard_map/pallas_call | solution.py:810
  83.5 0.0 collective-permute-done.sent_ref
  83.5 0.0 copy-start
  83.5 0.7 copy-done
  84.3 2.2 %shard_map.146 = (bf16[2,8,4608]{2,1,0:T(8,128)(2,1)}, bf16[2,8,4608]{2,1,0:T(8,128)(2,1)}) custom-call(bf16[4,8,4608]{2,1,0:T(8,128)(2,1)} %get-tuple-element.24.own_ref, bf16[4,8,4608]{2,1,0:T(8,128)(2,1)} %copy-done, bf16[2,8,4608]{2,1,0:T(8,128)(2,1)} %get-tuple-element.26.input_ref, bf16[2,8,4608]{2,1,0:T(8,128)(2,1)} %get-tuple-element.27.cot_ref, ...), custom_call_target="tpu_custom_call" | custom-call | tf_op jit(solution)/shard_map/pallas_call | solution.py:833
Async XLA Ops:
  73.4 10.1 %collective-permute-start = (bf16[4,8,4608]{2,1,0:T(8,128)(2,1)}, bf16[4,8,4608]{2,1,0:T(8,128)(2,1)S(1)}, u32[]{:S(2)}, u32[]{:S(2)}) collective-permute-start(bf16[4,8,4608]{2,1,0:T(8,128)(2,1)} %get-tuple-element.25), channel_id=1, source_target_pairs={{0,1},{1,0},{2,3},{3,2},{4,5},{5,4},{6,7},{7,6},{8,9},{9,8},{10,11... | collective-permute-start | bytes 884744 | tf_op jit(solution)/shard_map/ppermute | solution.py:15
  83.5 0.7 copy-start

commit v5 on v4

--- a/solution.py
+++ b/solution.py
@@ -158,6 +158,7 @@
 
 CHUNK = 512
 VMEM_GRANT = 60 * 1024 * 1024
+WHOLE_VMEM = 67043328
 MESH = pl.DeviceIdType.MESH
 
 
@@ -218,6 +219,8 @@
     targets_ref,
     wv,
     wo,
+    wv_turned,
+    wo_turned,
     xin,
     cot,
     staged,
@@ -243,6 +246,7 @@
     st_recv,
     side_send,
     side_recv,
+    gain_sems,
 ):
     s = lax.axis_index("section")
     d = lax.axis_index("dp")
@@ -312,7 +316,12 @@
             side_send.at[tick], side_recv.at[tick], (s, peer),
         )
 
-    gain_copy = remote(gain_send, gain_recv, side_send.at[0], side_recv.at[0], (s, peer))
+    def gain_copy(group):
+        return remote(
+            gain_send.at[group], gain_recv.at[group],
+            gain_sems.at[group, 0], gain_sems.at[group, 1], (s, peer),
+        )
+
     for stream in (0, 3, 1, 2):
         own_blocks[stream].wait()
         initial(stream).start()
@@ -392,12 +401,6 @@
         @pl.when(tick == 0)
         def _():
             weight_copies[key].wait()
-
-    def stash_sends(tick, group):
-        @pl.when(tick == ticks - 1)
-        def _():
-            for index in range(slots - 1):
-                stash_copy(index, group).start()
 
     def exchanged(tick, stream):
         going = tick < ticks - 1
@@ -459,25 +462,48 @@
         up_ref[group, tick] = whole(cot[tick, group]).astype(jnp.bfloat16)
         if group == 1:
             weights_ready(tick, (1, 1))
-        down = contract_sum(
-            width,
-            lambda at: times_transposed(up_ref[group, tick, :, at], wo[group, :, at]),
-            (rows, features),
-        ).astype(jnp.bfloat16)
-        down_ref[group, tick] = down
+            weights_ready(tick, (1, 0))
+
+        def products(out_turned, value_turned):
+            down = contract_sum(
+                width,
+                lambda at: jnp.dot(
+                    up_ref[group, tick, :, at], out_turned(at), preferred_element_type=jnp.float32
+                ),
+                (rows, features),
+            ).astype(jnp.bfloat16)
+            down_ref[group, tick] = down
+
+            def step(at):
+                psend[tick, 2 + group, :, :, at] = parted(
+                    jnp.dot(down, value_turned(at), preferred_element_type=jnp.float32)
+                )
+
+            chunk_loop(width, step)
+
+        def turn_out(at):
+            turned = wo[group, :, at].T
+            wo_turned[group, at, :] = turned
+            return turned
+
+        def turn_value(at):
+            turned = wv[group, at, :].T
+            wv_turned[group, :, at] = turned
+            return turned
+
+        @pl.when(tick == 0)
+        def _():
+            products(turn_out, turn_value)
+
+        @pl.when(tick > 0)
+        def _():
+            products(lambda at: wo_turned[group, at, :], lambda at: wv_turned[group, :, at])
+
+        @pl.when(exchanged(tick, 2 + group))
+        def _():
+            exchange(tick, 2 + group).start()
+
         if group == 1:
-            weights_ready(tick, (1, 0))
-
-        def step(at):
-            psend[tick, 2 + group, :, :, at] = parted(times_transposed(down, wv[group, at, :]))
-
-        chunk_loop(width, step)
-
-        @pl.when(exchanged(tick, 2 + group))
-        def _():
-            exchange(tick, 2 + group).start()
-
-        if group == 0:
             @pl.when((tick < ticks - 1) & (s == 0))
             def _():
                 fresh_copy(tick + 1).start()
@@ -539,10 +565,8 @@
         def _():
             backward_finish(tick - 1, 0)
 
-        stash_sends(tick, 1)
         forward_finish(tick, 0)
         forward_start(tick, 1)
-        stash_sends(tick, 0)
         own_source(tick, 1)
         backward_finish(tick, 1)
         backward_start(tick, 0)
@@ -550,14 +574,28 @@
         forward_finish(tick, 1)
         return None
 
-    lax.fori_loop(0, ticks, tick_step, None)
+    last = ticks - 1
+    lax.fori_loop(0, last, tick_step, None)
+    forward_start(last, 0)
+    backward_start(last, 1)
+
+    @pl.when(last > 0)
+    def _():
+        backward_finish(last - 1, 0)
+
+    for group in (1, 0):
+        for index in range(slots - 1):
+            stash_copy(index, group).start()
+    forward_start(last, 1)
+    own_source(last, 1)
+    backward_start(last, 0)
+    own_source(last, 0)
 
     def give(index, source, target):
         copy = pltpu.make_async_copy(source, target, out_sem.at[index])
         copy.start()
         return copy
 
-    last = ticks - 1
     given = [
         give(0, psend.at[last, :, 0], part_own_hbm),
         give(1, psend.at[last, :, 1], part_peer_hbm),
@@ -579,23 +617,25 @@
 
         lax.fori_loop(0, ticks, source_step, None)
         given.append(give(10 + group, normed_ref.at[group], normed_hbm.at[group]))
-        gain_send[pl.ds(group, 1), :] = jnp.sum(gain_sum[group], axis=0, keepdims=True)
-    gain_copy.start()
-    for group in range(2):
+        gain_send[group] = jnp.sum(gain_sum[group], axis=0, keepdims=True)
+        gain_copy(group).start()
+
         def chunk_values(at):
             block = normed_ref[group, :, :, :, at].astype(jnp.float32)
             left = block.reshape(ticks * rows, block.shape[3]).astype(jnp.bfloat16)
             return jnp.dot(left, wv[group, at, :], preferred_element_type=jnp.float32)
 
         vals_ref[group] = contract_sum(width, chunk_values, (ticks * rows, features)).astype(jnp.bfloat16)
-    given.append(give(12, vals_ref, vals_hbm))
-    gain_copy.wait_recv()
-    gain_sum[0, pl.ds(0, 2), :] = (gain_send[...] + gain_recv[...]) * (ticks * rows) ** (-0.5)
-    given.append(give(13, gain_sum.at[0, pl.ds(0, 2)], gain_hbm))
+        given.append(give(12 + group, vals_ref.at[group], vals_hbm.at[group]))
+    for group in (1, 0):
+        gain_copy(group).wait_recv()
+        gain_sum[0, pl.ds(group, 1), :] = (gain_send[group] + gain_recv[group]) * (ticks * rows) ** (-0.5)
+    given.append(give(14, gain_sum.at[0, pl.ds(0, 2)], gain_hbm))
     for copy in given:
         copy.wait()
 
-    gain_copy.wait_send()
+    for group in range(2):
+        gain_copy(group).wait_send()
     for stream in range(4):
         initial(stream).wait_send()
     for group in range(2):
@@ -771,6 +811,8 @@
             pltpu.VMEM((ticks, half, width), narrow),
             pltpu.VMEM(value_mats.shape, narrow),
             pltpu.VMEM(out_mats.shape, narrow),
+            pltpu.VMEM((2, features, width), narrow),
+            pltpu.VMEM((2, width, features), narrow),
             pltpu.VMEM((ticks, 3, 2, half, width), narrow),
             pltpu.VMEM((ticks, 2, 2, half, width), narrow),
             pltpu.VMEM((slots - 1, 2, half, width), narrow),
@@ -783,11 +825,11 @@
             pltpu.VMEM((2, half, width), jnp.float32),
             pltpu.VMEM((2, half, 128), jnp.float32),
             pltpu.VMEM((2, half, width), jnp.float32),
-            pltpu.VMEM((2, width), jnp.float32),
-            pltpu.VMEM((2, width), jnp.float32),
+            pltpu.VMEM((2, 1, width), jnp.float32),
+            pltpu.VMEM((2, 1, width), jnp.float32),
             pltpu.SemaphoreType.DMA((2, 2)),
             pltpu.SemaphoreType.DMA((7,)),
-            pltpu.SemaphoreType.DMA((14,)),
+            pltpu.SemaphoreType.DMA((15,)),
             pltpu.SemaphoreType.DMA((ticks, 4)),
             pltpu.SemaphoreType.DMA((ticks, 4)),
             pltpu.SemaphoreType.DMA((ticks, 4, 2)),
@@ -796,6 +838,7 @@
             pltpu.SemaphoreType.DMA((slots - 1, 2)),
             pltpu.SemaphoreType.DMA((ticks,)),
             pltpu.SemaphoreType.DMA((ticks,)),
+            pltpu.SemaphoreType.DMA((2, 2)),
         ],
         compiler_params=pltpu.CompilerParams(
             collective_id=0, has_side_effects=True, vmem_limit_bytes=VMEM_GRANT
@@ -825,7 +868,7 @@
             pltpu.SemaphoreType.DMA((2,)),
             pltpu.SemaphoreType.DMA((2,)),
         ],
-        compiler_params=pltpu.CompilerParams(vmem_limit_bytes=VMEM_GRANT),
+        compiler_params=pltpu.CompilerParams(vmem_limit_bytes=WHOLE_VMEM),
         cost_estimate=pl.CostEstimate(
             flops=32 * ticks * rows * width * features, bytes_accessed=8 * width * features, transcendentals=0
         ),

time: 86.7 us -> 81.6 us (0.941)
  Pallas kernels: 84.5 us -> 79.6 us
    pallas_call x1, Pallas kernels: 72.8 us -> 67.9 us  [relay_body(): pl.pallas_call(functools.partial(relay_kernel, sections), out_shape=(part...]
  transfers between devices with their start and end apart: 1 -> 1, of which waited for: 0 -> 0; matrix products, arithmetic and copies ran while one was open for 0% -> 0% of each run, Pallas kernels for 11% -> 12%
where the time goes in v5:
time: 81.6 us; the launch traced here: 81.3 us
  Pallas kernels  79.6 us (98%)
  starting transfers between devices  1.03 us (1%)
    pallas_call x1, Pallas kernels, relay_body(): pl.pallas_call(functools.partial(relay_kernel, sections), out_shape=(part...  67.9 us
    pallas_call x1, Pallas kernels, relay_body(): pl.pallas_call(functools.partial(grads_kernel, (ticks * rows) ** (-0.5)),...  9.52 us
    pallas_call x1, Pallas kernels, relay_body(): pl.pallas_call(final_kernel, out_shape=(shape(activations.shape, narrow),...  2.17 us
  transfers between devices with their start and end apart: 1, of which 0 were waited for; matrix products, arithmetic and copies ran while one was open for 0% of the time, Pallas kernels for 12%

profile of v5, /device:TPU:0, one launch (start us, length us, event | category | flops | bytes accessed | tf_op | source)
XLA Modules:
  0.0 81.3 jit_solution(5485441670566830972)
XLA Ops:
  0.6 67.9 %shard_map.145 = (bf16[4,8,4608]{2,1,0:T(8,128)(2,1)}, bf16[4,8,4608]{2,1,0:T(8,128)(2,1)}, bf16[2,8,4608]{2,1,0:T(8,128)(2,1)}, bf16[2,8,4608]{2,1,0:T(8,128)(2...) custom-call(bf16[2,4608,512]{2,1,0:T(8,128)(2,1)} %bitcast.21, ...), custom_call_target="tpu_custom_call" | custom-call | tf_op jit(solution)/shard_map/pallas_call | solution.py:787
  68.6 1.0 %collective-permute-start = (bf16[4,8,4608]{2,1,0:T(8,128)(2,1)}, bf16[4,8,4608]{2,1,0:T(8,128)(2,1)}, u32[]{:S(2)}, u32[]{:S(2)}) collective-permute-start(bf16[4,8,4608]{2,1,0:T(8,128)(2,1)} %get-tuple-element.25), channel_id=1, source_target_pairs={{0,1},{1,0},{2,3},{3,2},{4,5},{5,4},{6,7},{7,6},{8,9},{9,8},{10,11... | collective-permute-start | bytes 884744 | tf_op jit(solution)/shard_map/ppermute | solution.py:15
  69.6 9.5 %shard_map.147 = (bf16[3,2,8,4608]{3,2,1,0:T(8,128)(2,1)}, bf16[2,4608,512]{2,1,0:T(8,128)(2,1)}, bf16[2,512,4608]{2,1,0:T(8,128)(2,1)}, f32[2,4608]{1,0:T(2,128)}) custom-call(bf16[3,2,8,4608]{3,2,1,0:T(8,128)(2,1)} %get-tuple-element.32.stash_in, f32[2,4608]{1,0:T(2,128)} %get-tuple-element.33.gain_in, bf16[2,64,4608]{2,1,0:T(8,128)(2,1)} %bitcast.30, ...), custom_call_target="tpu_custom_call" | custom-call | flops 4831838208 | bytes 18874368 | tf_op jit(solution)/shard_map/pallas_call | solution.py:853
  79.1 0.0 collective-permute-done.sent_ref
  79.1 2.2 %shard_map.146 = (bf16[2,8,4608]{2,1,0:T(8,128)(2,1)}, bf16[2,8,4608]{2,1,0:T(8,128)(2,1)}) custom-call(bf16[4,8,4608]{2,1,0:T(8,128)(2,1)} %get-tuple-element.24.own_ref, bf16[4,8,4608]{2,1,0:T(8,128)(2,1)} %collective-permute-done.sent_ref, bf16[2,8,4608]{2,1,0:T(8,128)(2,1)} %get-tuple-element.26.input_ref, ...), custom_call_target="tpu_custom_call" | custom-call | tf_op jit(solution)/shard_map/pallas_call | solution.py:876
Async XLA Ops:
  68.6 10.6 %collective-permute-start = (bf16[4,8,4608]{2,1,0:T(8,128)(2,1)}, bf16[4,8,4608]{2,1,0:T(8,128)(2,1)}, u32[]{:S(2)}, u32[]{:S(2)}) collective-permute-start(bf16[4,8,4608]{2,1,0:T(8,128)(2,1)} %get-tuple-element.25), channel_id=1, source_target_pairs={{0,1},{1,0},{2,3},{3,2},{4,5},{5,4},{6,7},{7,6},{8,9},{9,8},{10,11... | collective-permute-start | bytes 884744 | tf_op jit(solution)/shard_map/ppermute | solution.py:15

commit v6 on v5

--- a/solution.py
+++ b/solution.py
@@ -442,8 +442,8 @@
             moved[tick, group] = outputs
 
             def send_on():
+                shift(tick, group, 0).start()
                 shift(tick, group, 1).start()
-                shift(tick, group, 0).start()
 
             if group == 0:
                 send_on()
@@ -554,8 +554,10 @@
             moved[tick, 2 + group] = input_gradient(
                 pulled, cot[tick, group, 0], scaled_own[group], root_own[group], gain_ref[pl.ds(group, 1), :]
             )
+            shift(tick, 2 + group, 0).start()
             shift(tick, 2 + group, 1).start()
-            shift(tick, 2 + group, 0).start()
+
+    last = ticks - 1
 
     def tick_step(tick, _):
         forward_start(tick, 0)
@@ -572,9 +574,14 @@
         backward_start(tick, 0)
         own_source(tick, 0)
         forward_finish(tick, 1)
+
+        @pl.when(tick == jnp.maximum(last - 1, 0))
+        def _():
+            for group in (1, 0):
+                for index in range(slots - 1):
+                    stash_copy(index, group).start()
         return None
 
-    last = ticks - 1
     lax.fori_loop(0, last, tick_step, None)
     forward_start(last, 0)
     backward_start(last, 1)
@@ -583,9 +590,6 @@
     def _():
         backward_finish(last - 1, 0)
 
-    for group in (1, 0):
-        for index in range(slots - 1):
-            stash_copy(index, group).start()
     forward_start(last, 1)
     own_source(last, 1)
     backward_start(last, 0)

time: 81.6 us -> 79.6 us (0.975)
  Pallas kernels: 79.6 us -> 78.3 us
    pallas_call x1, Pallas kernels: 67.9 us -> 66.6 us  [relay_body(): pl.pallas_call(functools.partial(relay_kernel, sections), out_shape=(part...]
where the time goes in v6:
time: 79.6 us; the launch traced here: 79.4 us
  Pallas kernels  78.3 us (98%)
    pallas_call x1, Pallas kernels, relay_body(): pl.pallas_call(functools.partial(relay_kernel, sections), out_shape=(part...  66.6 us
    pallas_call x1, Pallas kernels, relay_body(): pl.pallas_call(functools.partial(grads_kernel, (ticks * rows) ** (-0.5)),...  9.53 us
    pallas_call x1, Pallas kernels, relay_body(): pl.pallas_call(final_kernel, out_shape=(shape(activations.shape, narrow),...  2.17 us
  transfers between devices with their start and end apart: 1, of which 0 were waited for; matrix products, arithmetic and copies ran while one was open for 0% of the time, Pallas kernels for 12%

profile of v6, /device:TPU:0, one launch (start us, length us, event | category | flops | bytes accessed | tf_op | source)
XLA Modules:
  0.0 79.4 jit_solution(12386757717225212435)
XLA Ops:
  0.6 66.6 %shard_map.145 = (bf16[4,8,4608]{2,1,0:T(8,128)(2,1)}, bf16[4,8,4608]{2,1,0:T(8,128)(2,1)}, bf16[2,8,4608]{2,1,0:T(8,128)(2,1)}, bf16[2,8,4608]{2,1,0:T(8,128)(2...) custom-call(bf16[2,4608,512]{2,1,0:T(8,128)(2,1)} %bitcast.21, ...), custom_call_target="tpu_custom_call" | custom-call | tf_op jit(solution)/shard_map/pallas_call | solution.py:791
  67.3 0.4 collective-permute-start
  67.6 9.5 %shard_map.147 = (bf16[3,2,8,4608]{3,2,1,0:T(8,128)(2,1)}, bf16[2,4608,512]{2,1,0:T(8,128)(2,1)}, bf16[2,512,4608]{2,1,0:T(8,128)(2,1)}, f32[2,4608]{1,0:T(2,128)}) custom-call(bf16[3,2,8,4608]{3,2,1,0:T(8,128)(2,1)} %get-tuple-element.32.stash_in, f32[2,4608]{1,0:T(2,128)} %get-tuple-element.33.gain_in, bf16[2,64,4608]{2,1,0:T(8,128)(2,1)} %bitcast.30, ...), custom_call_target="tpu_custom_call" | custom-call | flops 4831838208 | bytes 18874368 | tf_op jit(solution)/shard_map/pallas_call | solution.py:857
  77.2 0.0 collective-permute-done.sent_ref
  77.2 2.2 %shard_map.146 = (bf16[2,8,4608]{2,1,0:T(8,128)(2,1)}, bf16[2,8,4608]{2,1,0:T(8,128)(2,1)}) custom-call(bf16[4,8,4608]{2,1,0:T(8,128)(2,1)} %get-tuple-element.24.own_ref, bf16[4,8,4608]{2,1,0:T(8,128)(2,1)} %collective-permute-done.sent_ref, bf16[2,8,4608]{2,1,0:T(8,128)(2,1)} %get-tuple-element.26.input_ref, ...), custom_call_target="tpu_custom_call" | custom-call | tf_op jit(solution)/shard_map/pallas_call | solution.py:880
Async XLA Ops:
  67.3 9.9 %collective-permute-start = (bf16[4,8,4608]{2,1,0:T(8,128)(2,1)}, bf16[4,8,4608]{2,1,0:T(8,128)(2,1)}, u32[]{:S(2)}, u32[]{:S(2)}) collective-permute-start(bf16[4,8,4608]{2,1,0:T(8,128)(2,1)} %get-tuple-element.25), channel_id=1, source_target_pairs={{0,1},{1,0},{2,3},{3,2},{4,5},{5,4},{6,7},{7,6},{8,9},{9,8},{10,11... | collective-permute-start | bytes 884744 | tf_op jit(solution)/shard_map/ppermute | solution.py:15
